TPU v7x, 32 devices: a whole 2x2x4 slice. The times are simulated.
32 devices in a mesh: expert: 4 (over z), tensor: 8 (over y, x, core).
Axes of the slice: x: 2, y: 2, z: 4, core: 2. Of those that a mesh axis runs over, the one named last changes fastest.
Arguments:
- layer_input: bfloat16 [8192, 2048], P('expert'), may hold values from -6 to 6
- cotangent: bfloat16 [8192, 2048], P(('expert', 'tensor')), may hold values from -6 to 6
- lengths: int32 [4, 4], P('expert'), may hold values from 1 to 1024, 2048 in all within a row
- routes: int32 [8192, 8], P(('expert', 'tensor')), may hold values from 0 to 15, all different within a row; in each aligned block of 256 rows (0 to 255, 256 to 511, ...) at most 192 rows name the same one
- attn_gain: float32 [2048], replicated, may hold values from 0.5 to 1.5
- w_qkv: bfloat16 [2048, 3, 2048], P(None, None, 'tensor'), may hold values from -0.125 to 0.125
- q_gain: float32 [128], replicated, may hold values from 0.6 to 5
- k_gain: float32 [128], replicated, may hold values from 0.6 to 5
- w_out: bfloat16 [2048, 2048], P('tensor'), may hold values from -2 to 2
- ffn_gain: float32 [2048], replicated, may hold values from 0.5 to 1.5
- w_router: bfloat16 [2048, 16], replicated, may hold values from -0.125 to 0.125
- w_gate: bfloat16 [16, 2048, 1024], P('expert', None, 'tensor'), may hold values from -0.125 to 0.125
- w_up: bfloat16 [16, 2048, 1024], P('expert', None, 'tensor'), may hold values from -0.125 to 0.125
- w_down: bfloat16 [16, 1024, 2048], P('expert', 'tensor'), may hold values from -6 to 6
Outputs:
- output: bfloat16 [8192, 2048], P(('expert', 'tensor'))
- grad_input: bfloat16 [8192, 2048], P(('expert', 'tensor'))
- grad_attn_gain: float32 [2048], replicated
- grad_w_qkv: float32 [2048, 3, 2048], P(None, None, 'tensor')
- grad_q_gain: float32 [128], replicated
- grad_k_gain: float32 [128], replicated
- grad_w_out: float32 [2048, 2048], P('tensor')
- grad_ffn_gain: float32 [2048], replicated
- grad_w_router: float32 [2048, 16], replicated
- grad_w_gate: float32 [16, 2048, 1024], P('expert', None, 'tensor')
- grad_w_up: float32 [16, 2048, 1024], P('expert', None, 'tensor')
- grad_w_down: float32 [16, 1024, 2048], P('expert', 'tensor')
Inputs may be any that keep to these rules, and one draw needn't show every extreme that they name: `routes`: no expert is named by more than 192 of the 256 rows of one device (aligned blocks of rows); in every draw some expert is named 192 times in some block. `lengths`: each row sums to 2048; its longest sequence has exactly 1024 tokens.
All inputs are finite; a program needn't handle non-finite values.
Results may differ from a plain program's by a relative error of at most 0.024.
The roundings to bfloat16 on the way count: a program that leaves them out, or rounds other values in their place, can miss the bound.
Values may be sent and summed in bfloat16 or wider, within the bound.
A program may use at most 384 MiB of HBM per device.

v0:
```python
import math

import jax
import jax.numpy as jnp
from jax import lax
from jax.sharding import PartitionSpec as P

NORM_EPS = 1e-06
ROPE_BASE = 50000.0


def rms_scale(values):
    return lax.rsqrt(jnp.mean(values * values, axis=-1, keepdims=True) + NORM_EPS)


def positions_of(seq_lengths, row_count):
    seq_ends = jnp.cumsum(seq_lengths)
    starts = seq_ends - seq_lengths
    row_index = jnp.arange(row_count, dtype=jnp.int32)
    segment = jnp.sum((row_index[:, None] >= seq_ends[None, :]).astype(jnp.int32), axis=1)
    picked = segment[:, None] == jnp.arange(seq_lengths.shape[0], dtype=jnp.int32)[None, :]
    offsets = jnp.sum(jnp.where(picked, starts[None, :], 0), axis=1)
    return (segment, row_index - offsets)


def rotate(values, position):
    half_width = values.shape[-1] // 2
    frequency = jnp.exp(
        jnp.arange(half_width, dtype=jnp.float32) * (-2.0 * math.log(ROPE_BASE) / values.shape[-1])
    )
    angle = position.astype(jnp.float32)[:, None] * frequency[None, :]
    cosine = jnp.cos(angle)[:, None, :]
    sine_part = jnp.sin(angle)[:, None, :]
    first_half = values[..., :half_width]
    second = values[..., half_width:]
    return jnp.concatenate(
        [first_half * cosine - second * sine_part, second * cosine + first_half * sine_part],
        axis=-1,
    )


def shape_heads(qkv_proj, q_gain, k_gain, position):
    query_rows = qkv_proj[:, 0]
    key_rows = qkv_proj[:, 1]
    value_rows = qkv_proj[:, 2]
    query_rows = rotate(query_rows * rms_scale(query_rows) * q_gain, position)
    key_rows = rotate(key_rows * rms_scale(key_rows) * k_gain, position)
    return (query_rows, key_rows, value_rows)


def masked_scores(query_block, key_rows, segment_block, segment, score_scale):
    scores = (
        jnp.einsum("qhd,khd->hqk", query_block, key_rows, preferred_element_type=jnp.float32)
        * score_scale
    )
    same_seq = (segment_block[:, None] == segment[None, :])[None]
    return jnp.where(same_seq, scores, -1e30)


def attend_forward(query_rows, key_rows, value_rows, segment, block_rows, score_scale):
    row_count, head_count, head_width = query_rows.shape
    block_count = row_count // block_rows

    def one_block(block_item):
        query_block, segment_block = block_item
        scores = masked_scores(query_block, key_rows, segment_block, segment, score_scale)
        row_peak = jnp.max(scores, axis=-1, keepdims=True)
        weights = jnp.exp(scores - row_peak)
        row_total = jnp.sum(weights, axis=-1, keepdims=True)
        probabilities = (weights / row_total).astype(jnp.bfloat16)
        mixed_out = jnp.einsum(
            "hqk,khd->qhd", probabilities, value_rows, preferred_element_type=jnp.float32
        )
        return (mixed_out, (row_peak + jnp.log(row_total))[..., 0])

    blocks = (
        query_rows.reshape(block_count, block_rows, head_count, head_width),
        segment.reshape(block_count, block_rows),
    )
    mixed_out, log_total = lax.map(one_block, blocks)
    return (mixed_out.reshape(row_count, head_count, head_width), log_total)


def attend_backward(
    query_rows, key_rows, value_rows, segment, grad_mixed, log_total, block_rows, score_scale
):
    row_count, head_count, head_width = query_rows.shape
    block_count = row_count // block_rows

    def one_block(carry, block_item):
        grad_keys, grad_values = carry
        query_block, segment_block, grad_block, total_block = block_item
        scores = masked_scores(query_block, key_rows, segment_block, segment, score_scale)
        probabilities = jnp.exp(scores - total_block[..., None])
        grad_probs = jnp.einsum(
            "qhd,khd->hqk", grad_block, value_rows, preferred_element_type=jnp.float32
        )
        delta = jnp.sum(grad_probs * probabilities, axis=-1, keepdims=True)
        grad_scores = (probabilities * (grad_probs - delta)).astype(jnp.bfloat16)
        grad_query = (
            jnp.einsum("hqk,khd->qhd", grad_scores, key_rows, preferred_element_type=jnp.float32)
            * score_scale
        )
        grad_keys = (
            grad_keys
            + jnp.einsum(
                "hqk,qhd->khd", grad_scores, query_block, preferred_element_type=jnp.float32
            )
            * score_scale
        )
        grad_values = grad_values + jnp.einsum(
            "hqk,qhd->khd",
            probabilities.astype(jnp.bfloat16),
            grad_block,
            preferred_element_type=jnp.float32,
        )
        return ((grad_keys, grad_values), grad_query)

    blocks = (
        query_rows.reshape(block_count, block_rows, head_count, head_width),
        segment.reshape(block_count, block_rows),
        grad_mixed.reshape(block_count, block_rows, head_count, head_width),
        log_total,
    )
    start_carry = (jnp.zeros(key_rows.shape, jnp.float32), jnp.zeros(value_rows.shape, jnp.float32))
    (grad_keys, grad_values), grad_query = lax.scan(one_block, start_carry, blocks)
    return (grad_query.reshape(row_count, head_count, head_width), grad_keys, grad_values)


def swiglu_back(grad_hidden, gate_pre, up_pre):
    sigmoid = jax.nn.sigmoid(gate_pre)
    grad_gate = grad_hidden * up_pre * sigmoid * (1.0 + gate_pre * (1.0 - sigmoid))
    grad_up = grad_hidden * gate_pre * sigmoid
    return (grad_gate.astype(jnp.bfloat16), grad_up.astype(jnp.bfloat16))


def body(
    layer_input,
    cotangent,
    lengths,
    routes,
    attn_gain,
    w_qkv,
    q_gain,
    k_gain,
    w_out,
    ffn_gain,
    w_router,
    w_gate,
    w_up,
    w_down,
):
    group_rows, model_width = layer_input.shape
    own_rows, top_count = routes.shape
    head_width = q_gain.shape[0]
    local_heads = w_qkv.shape[2] // head_width
    experts_all = w_router.shape[1]
    experts_here = w_gate.shape[0]
    senders = lax.axis_size("expert")
    tensor_rank = lax.axis_index("tensor")
    capacity = max(2, 3 * own_rows * top_count // (2 * experts_all))
    block_rows = min(512, group_rows)
    score_scale = 1.0 / math.sqrt(head_width)
    input_full = layer_input.astype(jnp.float32)
    scale_one = rms_scale(input_full)
    normed = (input_full * scale_one * attn_gain).astype(jnp.bfloat16)
    qkv_weight = w_qkv.reshape(model_width, 3 * local_heads * head_width)
    qkv_proj = jnp.dot(normed, qkv_weight, preferred_element_type=jnp.float32).reshape(
        group_rows, 3, local_heads, head_width
    )
    segment, position = positions_of(lengths[0], group_rows)

    def head_shapes(raw_proj, gain_q, gain_k):
        return shape_heads(raw_proj, gain_q, gain_k, position)

    (query_full, key_full, value_full), head_back = jax.vjp(head_shapes, qkv_proj, q_gain, k_gain)
    query_low = query_full.astype(jnp.bfloat16)
    key_low = key_full.astype(jnp.bfloat16)
    value_low = value_full.astype(jnp.bfloat16)
    mixed_full, log_total = attend_forward(
        query_low, key_low, value_low, segment, block_rows, score_scale
    )
    mixed_low = mixed_full.astype(jnp.bfloat16).reshape(group_rows, local_heads * head_width)
    row_part = mixed_low
    attn_own = lax.psum_scatter(
        jnp.dot(row_part, w_out, preferred_element_type=jnp.float32),
        "tensor",
        scatter_dimension=0,
        tiled=True,
    )
    input_own = lax.dynamic_slice_in_dim(input_full, tensor_rank * own_rows, own_rows, 0)
    scale_own = lax.dynamic_slice_in_dim(scale_one, tensor_rank * own_rows, own_rows, 0)
    residual = input_own + attn_own
    scale_two = rms_scale(residual)
    ffn_in = (residual * scale_two * ffn_gain).astype(jnp.bfloat16)
    logits = jnp.dot(ffn_in, w_router, preferred_element_type=jnp.float32)
    probabilities = jax.nn.softmax(logits, axis=-1)
    chosen = routes[:, :, None] == jnp.arange(experts_all, dtype=jnp.int32)[None, None, :]
    gate_weights = jnp.sum(jnp.where(chosen, probabilities[:, None, :], 0.0), axis=-1)
    grad_output = cotangent.astype(jnp.float32)
    flat_routes = routes.reshape(-1)
    expert_hits = (
        flat_routes[:, None] == jnp.arange(experts_all, dtype=jnp.int32)[None, :]
    ).astype(jnp.int32)
    slot_index = jnp.sum(expert_hits * (jnp.cumsum(expert_hits, axis=0) - 1), axis=1)
    spread_in = jnp.broadcast_to(ffn_in[:, None, :], (own_rows, top_count, model_width)).reshape(
        -1, model_width
    )
    spread_grad = (
        (gate_weights[:, :, None] * grad_output[:, None, :])
        .astype(jnp.bfloat16)
        .reshape(-1, model_width)
    )
    send_in = (
        jnp.zeros((experts_all, capacity, model_width), jnp.bfloat16)
        .at[flat_routes, slot_index]
        .set(spread_in)
    )
    send_grad = (
        jnp.zeros((experts_all, capacity, model_width), jnp.bfloat16)
        .at[flat_routes, slot_index]
        .set(spread_grad)
    )
    layout = (senders, experts_here, capacity, model_width)
    recv_rows, expert_grad = (
        lax.all_to_all(send_in.reshape(layout), "expert", split_axis=0, concat_axis=0, tiled=True),
        lax.all_to_all(
            send_grad.reshape(layout), "expert", split_axis=0, concat_axis=0, tiled=True
        ),
    )
    gate_full, up_full, down_full = (
        lax.all_gather(w_gate, "tensor", axis=2, tiled=True),
        lax.all_gather(w_up, "tensor", axis=2, tiled=True),
        lax.all_gather(w_down, "tensor", axis=1, tiled=True),
    )
    gate_all = jnp.einsum(
        "sctd,cdf->sctf", recv_rows, gate_full, preferred_element_type=jnp.float32
    )
    up_all = jnp.einsum("sctd,cdf->sctf", recv_rows, up_full, preferred_element_type=jnp.float32)
    hidden_low = (jax.nn.silu(gate_all) * up_all).astype(jnp.bfloat16)
    expert_out = jnp.einsum(
        "sctf,cfd->sctd", hidden_low, down_full, preferred_element_type=jnp.float32
    ).astype(jnp.bfloat16)
    grad_hidden = jnp.einsum(
        "sctd,cfd->sctf", expert_grad, down_full, preferred_element_type=jnp.float32
    )
    grad_gate_pre, grad_up_pre = swiglu_back(grad_hidden, gate_all, up_all)
    whole_down = jnp.einsum(
        "sctf,sctd->cfd", hidden_low, expert_grad, preferred_element_type=jnp.float32
    )
    whole_gate = jnp.einsum(
        "sctd,sctf->cdf", recv_rows, grad_gate_pre, preferred_element_type=jnp.float32
    )
    whole_up = jnp.einsum(
        "sctd,sctf->cdf", recv_rows, grad_up_pre, preferred_element_type=jnp.float32
    )
    from_gate = jnp.einsum(
        "sctf,cdf->sctd", grad_gate_pre, gate_full, preferred_element_type=jnp.float32
    )
    from_up = jnp.einsum("sctf,cdf->sctd", grad_up_pre, up_full, preferred_element_type=jnp.float32)
    grad_inputs = (from_gate + from_up).astype(jnp.bfloat16)
    grad_gate, grad_up, grad_down = (
        lax.psum_scatter(
            whole_gate.astype(jnp.bfloat16), "tensor", scatter_dimension=2, tiled=True
        ).astype(jnp.float32),
        lax.psum_scatter(
            whole_up.astype(jnp.bfloat16), "tensor", scatter_dimension=2, tiled=True
        ).astype(jnp.float32),
        lax.psum_scatter(
            whole_down.astype(jnp.bfloat16), "tensor", scatter_dimension=1, tiled=True
        ).astype(jnp.float32),
    )
    back_rows, back_grads = (
        lax.all_to_all(expert_out, "expert", split_axis=0, concat_axis=0, tiled=True),
        lax.all_to_all(grad_inputs, "expert", split_axis=0, concat_axis=0, tiled=True),
    )
    pick_index = flat_routes * capacity + slot_index
    rows_back = (
        back_rows.reshape(experts_all * capacity, model_width)[pick_index]
        .reshape(own_rows, top_count, model_width)
        .astype(jnp.float32)
    )
    grads_back = (
        back_grads.reshape(experts_all * capacity, model_width)[pick_index]
        .reshape(own_rows, top_count, model_width)
        .astype(jnp.float32)
    )
    mixture = jnp.sum(gate_weights[:, :, None] * rows_back, axis=1)
    output = (residual + mixture).astype(jnp.bfloat16)
    grad_gates = jnp.sum(grad_output[:, None, :] * rows_back, axis=-1)
    grad_probs = jnp.sum(jnp.where(chosen, grad_gates[:, :, None], 0.0), axis=1)
    grad_logits = (
        probabilities * (grad_probs - jnp.sum(grad_probs * probabilities, axis=-1, keepdims=True))
    ).astype(jnp.bfloat16)
    router_part = lax.dot_general(
        ffn_in, grad_logits, (((0,), (0,)), ((), ())), preferred_element_type=jnp.float32
    )
    grad_ffn = jnp.sum(grads_back, axis=1) + lax.dot_general(
        grad_logits, w_router, (((1,), (1,)), ((), ())), preferred_element_type=jnp.float32
    )
    ffn_gain_part = jnp.sum(grad_ffn * residual * scale_two, axis=0)
    scaled_two = grad_ffn * ffn_gain
    grad_residual = grad_output + scale_two * (
        scaled_two
        - residual * scale_two * scale_two * jnp.mean(scaled_two * residual, axis=-1, keepdims=True)
    )
    grad_attn = grad_residual.astype(jnp.bfloat16)
    shard_part = lax.all_gather(grad_attn, "tensor", axis=0, tiled=True)
    grad_weight = lax.dot_general(
        mixed_low, shard_part, (((0,), (0,)), ((), ())), preferred_element_type=jnp.float32
    )
    grad_rows_part = lax.dot_general(
        shard_part, w_out, (((1,), (1,)), ((), ())), preferred_element_type=jnp.float32
    ).astype(jnp.bfloat16)
    grad_mixed = grad_rows_part
    out_part, grad_mixed = (grad_weight, grad_mixed)
    grad_query, grad_keys, grad_values = attend_backward(
        query_low,
        key_low,
        value_low,
        segment,
        grad_mixed.reshape(group_rows, local_heads, head_width),
        log_total,
        block_rows,
        score_scale,
    )
    grad_qkv, q_gain_part, k_gain_part = head_back((grad_query, grad_keys, grad_values))
    grad_qkv_low = grad_qkv.astype(jnp.bfloat16).reshape(group_rows, 3 * local_heads * head_width)
    qkv_part = lax.dot_general(
        normed, grad_qkv_low, (((0,), (0,)), ((), ())), preferred_element_type=jnp.float32
    ).reshape(w_qkv.shape)
    row_part = grad_qkv_low
    grad_normed = lax.psum_scatter(
        lax.dot_general(
            row_part, qkv_weight, (((1,), (1,)), ((), ())), preferred_element_type=jnp.float32
        ).astype(jnp.bfloat16),
        "tensor",
        scatter_dimension=0,
        tiled=True,
    ).astype(jnp.float32)
    attn_gain_part = jnp.sum(grad_normed * input_own * scale_own, axis=0)
    scaled_one = grad_normed * attn_gain
    grad_input = grad_residual + scale_own * (
        scaled_one
        - input_own
        * scale_own
        * scale_own
        * jnp.mean(scaled_one * input_own, axis=-1, keepdims=True)
    )
    grad_qkv_sum, grad_out_sum = (
        lax.psum(qkv_part.astype(jnp.bfloat16), "expert").astype(jnp.float32),
        lax.psum(out_part.astype(jnp.bfloat16), "expert").astype(jnp.float32),
    )
    grad_attn_gain, grad_q_gain, grad_k_gain, grad_ffn_gain, grad_router = lax.psum(
        (attn_gain_part, q_gain_part, k_gain_part, ffn_gain_part, router_part), ("expert", "tensor")
    )
    return (
        output,
        grad_input.astype(jnp.bfloat16),
        grad_attn_gain,
        grad_qkv_sum,
        grad_q_gain,
        grad_k_gain,
        grad_out_sum,
        grad_ffn_gain,
        grad_router,
        grad_gate,
        grad_up,
        grad_down,
    )


def solution(mesh):
    in_specs = (
        P("expert", None),
        P(("expert", "tensor"), None),
        P("expert", None),
        P(("expert", "tensor"), None),
        P(),
        P(None, None, "tensor"),
        P(),
        P(),
        P("tensor", None),
        P(),
        P(),
        P("expert", None, "tensor"),
        P("expert", None, "tensor"),
        P("expert", "tensor", None),
    )
    out_specs = (
        P(("expert", "tensor"), None),
        P(("expert", "tensor"), None),
        P(),
        P(None, None, "tensor"),
        P(),
        P(),
        P("tensor", None),
        P(),
        P(),
        P("expert", None, "tensor"),
        P("expert", None, "tensor"),
        P("expert", "tensor", None),
    )
    return jax.shard_map(body, mesh=mesh, in_specs=in_specs, out_specs=out_specs, check_vma=False)
```

profile of v0, /device:TPU:0, one launch (start us, length us, event | category | flops | bytes accessed | tf_op | source)
XLA Modules:
  0.0 2259.6 jit_solution(2812571986861035458)
XLA Ops:
  49.6 41.2 %while.27 = (s32[]{:T(128)}, bf16[4,512,2,128]{3,1,2,0:T(8,128)(2,1)}, f32[4,2,512]{2,1,0:T(2,128)}, s32[4,512]{1,0:T(4,128)S(1)}, s32[2048]{0:T(1024)S(1)}, /*i...) while((s32[]{:T(128)}, ...), condition=%wide.region_9.10_spmd, body=%wide.region_6.9_spmd.sunk | while | flops 1099955200 | bytes 32292448 | solution.py:80
  104.7 14.1 convert_element_type.146
  125.6 96.5 %reduce-scatter.10.cloned.1.call-done = f32[256,2048]{1,0:T(8,128)} async-done(((f32[2048,2048]{1,0:T(8,128)}), f32[256,2048]{1,0:T(8,128)}) %reduce-scatter.10.cloned.1.call-update) | async-done | bytes 2097168 | tf_op jit(solution)/shard_map/reduce_scatter | solution.py:185
  226.3 19.1 scatter_custom_fusion
  257.2 19.8 scatter_custom_fusion.1
  277.0 247.9 %all-to-all-done = bf16[4,4,192,2048]{3,2,1,0:T(8,128)(2,1)} async-done(((bf16[4,4,192,2048]{3,2,1,0:T(8,128)(2,1)}), bf16[4,4,192,2048]{3,2,1,0:T(8,128)(2,1)}, u32[]{:S(2)}, u32[]{:S(2)}) %all-to-all-start) | async-done | bytes 12582944 | tf_op jit(solution)/shard_map/all_to_all | solution.py:226
  531.7 22.6 %fusion.42 = f32[4,4,192,1024]{3,2,1,0:T(8,128)} fusion(bf16[4,2048,1024]{2,1,0:T(8,128)(2,1)} %all-gather.5.cloned.1.call-done, bf16[4,4,192,2048]{3,2,1,0:T(8,128)(2,1)} %all-to-all-done), kind=kOutput, calls=%fused_computation.64 | convolution fusion | flops 12884901888 | bytes 41943040 | tf_op jit(solution)/shard_map/sctd,cdf->sctf/dot_general | solution.py:236
  554.4 22.6 %fusion.38 = f32[4,4,192,1024]{3,2,1,0:T(8,128)} fusion(bf16[4,2048,1024]{2,1,0:T(8,128)(2,1)} %all-gather.7.cloned.1.call-done, bf16[4,4,192,2048]{3,2,1,0:T(8,128)(2,1)} %all-to-all-done), kind=kOutput, calls=%fused_computation.60 | convolution fusion | flops 12884901888 | bytes 41943040 | tf_op jit(solution)/shard_map/sctd,cdf->sctf/dot_general | solution.py:239
  577.0 227.2 %all-to-all-done.2 = bf16[4,4,192,2048]{3,2,1,0:T(8,128)(2,1)} async-done(((bf16[4,4,192,2048]{3,2,1,0:T(8,128)(2,1)}), bf16[4,4,192,2048]{3,2,1,0:T(8,128)(2,1)}, u32[]{:S(2)}, u32[]{:S(2)}) %all-to-all-start.2) | async-done | bytes 12582944 | tf_op jit(solution)/shard_map/all_to_all | solution.py:227
  804.2 31.3 %fusion.52 = (bf16[4,4,192,1024]{3,2,0,1:T(8,128)(2,1)}, bf16[4,4,192,1024]{3,2,0,1:T(8,128)(2,1)}, bf16[4,4,192,1024]{3,2,0,1:T(8,128)(2,1)}) fusion(f32[4,4,192,1024]{3,2,1,0:T(8,128)} %fusion.38, f32[4,4,192,1024]{3,2,1,0:T(8,128)} %fusion.42, bf16[4,1024,2048]{2,1,0:T(8,128)(2,1)} %all-gather.9.cloned.1.call-done, ...), kind=kOutput, calls=%fused_computation.79 | convolution fusion | flops 12935233536 | bytes 73400320 | tf_op jit(solution)/shard_map/sctd,cfd->sctf/dot_general | solution.py:244
  835.5 22.9 %convert_bitcast_fusion = bf16[4,4,192,2048]{3,2,0,1:T(8,128)(2,1)} fusion(bf16[4,4,192,1024]{3,2,0,1:T(8,128)(2,1)} %get-tuple-element.315, bf16[4,1024,2048]{2,1,0:T(8,128)(2,1)} %all-gather.9.cloned.1.call-done), kind=kOutput, calls=%fused_computation.91 | convolution fusion | flops 12891193344 | bytes 35651584 | tf_op jit(solution)/shard_map/sctf,cfd->sctd/dot_general | solution.py:241
  875.5 21.8 fusion.36
  897.3 24.3 %fusion.49 = bf16[4,4,192,2048]{3,2,0,1:T(8,128)(2,1)} fusion(f32[4,4,192,2048]{3,2,1,0:T(8,128)} %fusion.36, bf16[4,4,192,1024]{3,2,0,1:T(8,128)(2,1)} %get-tuple-element.314, bf16[4,2048,1024]{2,1,0:T(8,128)(2,1)} %all-gather.5.cloned.1.call-done), kind=kOutput, calls=%fused_computation.74 | convolution fusion | flops 12897484800 | bytes 60817408 | tf_op jit(solution)/shard_map/sctf,cdf->sctd/dot_general | solution.py:257
  932.3 215.7 %all-to-all-done.1 = bf16[4,4,192,2048]{3,2,1,0:T(8,128)(2,1)} async-done(((bf16[4,4,192,2048]{3,2,1,0:T(8,128)(2,1)}), bf16[4,4,192,2048]{3,2,1,0:T(8,128)(2,1)}, u32[]{:S(2)}, u32[]{:S(2)}) %all-to-all-start.1) | async-done | bytes 12582944 | tf_op jit(solution)/shard_map/all_to_all | solution.py:274
  1154.4 22.9 %gather_fusion = bf16[2048,2048]{1,0:T(8,128)(2,1)} fusion(bf16[3072,2048]{1,0:T(8,128)(2,1)} %bitcast.30, s32[2048]{0:T(1024)S(1)} %broadcast_clamp_fusion), kind=kCustom, calls=%fused_computation | custom fusion | bytes 16785408 | tf_op jit(solution)/shard_map/gather | solution.py:279
  1187.0 239.8 %all-to-all-done.3 = bf16[4,4,192,2048]{3,2,1,0:T(8,128)(2,1)} async-done(((bf16[4,4,192,2048]{3,2,1,0:T(8,128)(2,1)}), bf16[4,4,192,2048]{3,2,1,0:T(8,128)(2,1)}, u32[]{:S(2)}, u32[]{:S(2)}) %all-to-all-start.3) | async-done | bytes 12582944 | tf_op jit(solution)/shard_map/all_to_all | solution.py:275
  1426.8 22.9 %gather_fusion.1 = bf16[2048,2048]{1,0:T(8,128)(2,1)} fusion(bf16[3072,2048]{1,0:T(8,128)(2,1)} %bitcast.40, s32[2048]{0:T(1024)S(1)} %broadcast_clamp_fusion), kind=kCustom, calls=%fused_computation.1 | custom fusion | bytes 16785408 | tf_op jit(solution)/shard_map/gather | solution.py:284
  1449.8 11.4 convert_reduce_fusion
  1467.4 19.8 bitcast_convert_fusion.2
  1487.2 28.9 %copy.149 = bf16[4,2048,1024]{1,0,2:T(4,128)(2,1)} copy(bf16[4,2048,1024]{2,1,0:T(8,128)(2,1)} %bitcast_convert_fusion.2) | data formatting | bytes 33554432
  1516.0 18.6 copy.184
  1534.7 20.5 bitcast_convert_fusion.1
  1555.2 29.2 %copy.151 = bf16[4,2048,1024]{1,0,2:T(4,128)(2,1)} copy(bf16[4,2048,1024]{2,1,0:T(8,128)(2,1)} %bitcast_convert_fusion.1) | data formatting | bytes 33554432
  1584.4 18.9 copy.185
  1603.4 21.6 bitcast_convert_fusion
  1632.1 165.0 %while.28 = (s32[]{:T(128)}, f32[2048,2,128]{0,2,1:T(8,128)}, f32[2048,2,128]{0,2,1:T(8,128)}, f32[4,512,2,128]{1,0,3,2:T(4,128)}, bf16[4,512,2,128]{3,1,2,0:T(8...) while((s32[]{:T(128)}, f32[2048,2,128]{0,2,1:T(8,128)}, ...), condition=%wide.region_28.29_spmd.clone, body=%wide.region_26.28_spmd.clone.sunk | while | flops 2719611904 | bytes 170962192 | solution.py:126
  1824.8 11.8 convolution_convert_fusion
  1859.3 29.5 %reduce-scatter.14.cloned.1.call-done = bf16[4,128,2048]{2,1,0:T(8,128)(2,1)} async-done(((bf16[4,1024,2048]{2,1,0:T(8,128)(2,1)}), bf16[4,128,2048]{2,1,0:T(8,128)(2,1)}) %reduce-scatter.14.cloned.1.call-update) | async-done | bytes 2097168 | tf_op jit(solution)/shard_map/reduce_scatter | solution.py:269
  1892.9 153.9 %all-reduce.14.cloned.1.call-done = (bf16[2048,3,256]{2,0,1:T(8,128)(2,1)}, bf16[256,2048]{1,0:T(8,128)(2,1)}) async-done(((bf16[2048,3,256]{2,0,1:T(8,128)(2,1)}, bf16[256,2048]{1,0:T(8,128)(2,1)}), (bf16[2048,3,256]{2,0,1:T(8,128)(2,1)}, bf16[256,2048]{1,0:T(8,128)(2,1)})) %all-reduce.14.cloned.1.call-update) | async-done | bytes 4194320 | tf_op jit(solution)/shard_map/psum | solution.py:351
  2053.7 67.0 %reduce-scatter.12.cloned.1.call-done = bf16[256,2048]{1,0:T(8,128)(2,1)} async-done(((bf16[2048,2048]{1,0:T(8,128)(2,1)}), bf16[256,2048]{1,0:T(8,128)(2,1)}) %reduce-scatter.12.cloned.1.call-update) | async-done | bytes 1048592 | tf_op jit(solution)/shard_map/reduce_scatter | solution.py:333
  2129.3 39.8 %all-reduce.7 = (f32[2048]{0:T(1024)}, f32[128]{0:T(128)}, f32[128]{0:T(128)}, f32[2048]{0:T(1024)}) all-reduce(f32[2048]{0:T(1024)S(1)} %get-tuple-element.250, f32[128]{0:T(128)S(1)} %get-tuple-element.259, f32[128]{0:T(128)S(1)} %get-tuple-element.252, ...), channel_id=1, replica_groups=mesh['expert'=4,'tensor'=8] {'expert','tensor'}, use_global_device_ids=true, to_apply=%region_34.35 | all-reduce | flops 4352 | bytes 34816 | tf_op jit(solution)/shard_map/psum | solution.py:354
  2169.0 82.2 %all-reduce.12.cloned.1.call-done = f32[2048,16]{0,1:T(8,128)} async-done(((f32[2048,16]{0,1:T(8,128)}), f32[2048,16]{0,1:T(8,128)}) %all-reduce.12.cloned.1.call-update) | async-done | bytes 131088 | tf_op jit(solution)/shard_map/psum | solution.py:354
  (376 shorter events, 419.2 us)
Async XLA Ops:
  7.2 87.8 %copy-start = (bf16[256,2048]{1,0:T(8,128)(2,1)S(1)}, bf16[256,2048]{1,0:T(8,128)(2,1)}, u32[]{:S(2)}) copy-start(bf16[256,2048]{1,0:T(8,128)(2,1)} %param.26) | copy-start | bytes 3145732
  7.2 215.0 %reduce-scatter.10.cloned.1.call-start = ((), (), s32[]{:S(2)}) async-start(), calls=%async_computation.9 | async-start | bytes 18874368 | tf_op jit(solution)/shard_map/reduce_scatter | solution.py:185
  103.1 428.6 %all-gather.5.cloned.1.call-start = ((), (), s32[]{:S(2)}) async-start(), calls=%async_computation.10 | async-start | bytes 18874368 | tf_op jit(solution)/shard_map/all_gather | solution.py:232
  103.9 450.5 %all-gather.7.cloned.1.call-start = ((), (), s32[]{:S(2)}) async-start(), calls=%async_computation.11 | async-start | bytes 18874368 | tf_op jit(solution)/shard_map/all_gather | solution.py:233
  104.6 20.8 copy-start.68
  104.7 20.8 copy-start.67
  118.8 107.3 %copy-start.40 = (f32[2048]{0:T(1024)S(1)}, f32[2048]{0:T(1024)}, u32[]{:S(2)}) copy-start(f32[2048]{0:T(1024)} %param.27) | copy-start | bytes 24580
  224.7 20.7 copy-start.52
  226.3 19.1 copy-start.15
  245.4 279.5 %all-to-all-start = ((bf16[4,4,192,2048]{3,2,1,0:T(8,128)(2,1)}), bf16[4,4,192,2048]{3,2,1,0:T(8,128)(2,1)}, u32[]{:S(2)}, u32[]{:S(2)}) async-start(bf16[4,4,192,2048]{3,2,1,0:T(8,128)(2,1)} %bitcast.307), calls=%async_computation.1 | async-start | bytes 25165824 | tf_op jit(solution)/shard_map/all_to_all | solution.py:226
  251.8 325.1 %all-gather.9.cloned.1.call-start = ((), (), s32[]{:S(2)}) async-start(), calls=%async_computation.12 | async-start | bytes 18874368 | tf_op jit(solution)/shard_map/all_gather | solution.py:234
  253.9 23.1 %copy-start.13 = (f32[256,2048]{1,0:T(8,128)}, f32[256,2048]{1,0:T(8,128)S(1)}, u32[]{:S(2)}) copy-start(f32[256,2048]{1,0:T(8,128)S(1)} %convert_element_type.161) | copy-start | bytes 6291460
  257.1 19.9 copy-start.25
  524.9 279.3 %all-to-all-start.2 = ((bf16[4,4,192,2048]{3,2,1,0:T(8,128)(2,1)}), bf16[4,4,192,2048]{3,2,1,0:T(8,128)(2,1)}, u32[]{:S(2)}, u32[]{:S(2)}) async-start(bf16[4,4,192,2048]{3,2,1,0:T(8,128)(2,1)} %bitcast.308), calls=%async_computation.3 | async-start | bytes 25165824 | tf_op jit(solution)/shard_map/all_to_all | solution.py:227
  869.2 278.8 %all-to-all-start.1 = ((bf16[4,4,192,2048]{3,2,1,0:T(8,128)(2,1)}), bf16[4,4,192,2048]{3,2,1,0:T(8,128)(2,1)}, u32[]{:S(2)}, u32[]{:S(2)}) async-start(bf16[4,4,192,2048]{3,2,1,0:T(8,128)(2,1)} %copy.127), calls=%async_computation.2 | async-start | bytes 25165824 | tf_op jit(solution)/shard_map/all_to_all | solution.py:274
  932.3 222.1 %copy-start.51 = (s32[2048,1]{0,1:T(1,128)S(1)}, s32[2048,1]{0,1:T(1,128)}, u32[]{:S(2)}) copy-start(s32[2048,1]{0,1:T(1,128)} %get-tuple-element.337) | copy-start | bytes 24580
  1148.0 278.8 %all-to-all-start.3 = ((bf16[4,4,192,2048]{3,2,1,0:T(8,128)(2,1)}), bf16[4,4,192,2048]{3,2,1,0:T(8,128)(2,1)}, u32[]{:S(2)}, u32[]{:S(2)}) async-start(bf16[4,4,192,2048]{3,2,1,0:T(8,128)(2,1)} %copy.130), calls=%async_computation.4 | async-start | bytes 25165824 | tf_op jit(solution)/shard_map/all_to_all | solution.py:275
  1154.3 470.8 %all-gather.11.cloned.1.call-start = ((), (), s32[]{:S(2)}) async-start(), calls=%async_computation.13 | async-start | bytes 9437184 | tf_op jit(solution)/shard_map/all_gather | solution.py:308
  1154.4 22.9 %copy-start.14 = (f32[256,2048]{1,0:T(8,128)S(1)}, f32[256,2048]{1,0:T(8,128)}, u32[]{:S(2)}) copy-start(f32[256,2048]{1,0:T(8,128)} %copy-done.13) | copy-start | bytes 6291460
  1154.4 22.9 %copy-start.26 = (f32[256,8]{1,0:T(8,128)S(1)}, f32[256,8]{1,0:T(8,128)}, u32[]{:S(2)}) copy-start(f32[256,8]{1,0:T(8,128)} %copy-done.25) | copy-start | bytes 24580
  1187.0 274.3 %copy-start.44 = (bf16[256,16]{0,1:T(8,128)(2,1)}, bf16[256,16]{0,1:T(8,128)(2,1)S(1)}, u32[]{:S(2)}) copy-start(bf16[256,16]{0,1:T(8,128)(2,1)S(1)} %multiply_convert_fusion.5) | copy-start | bytes 24580
  1464.3 22.8 %copy-start.61 = (f32[256]{0:T(256)}, f32[256]{0:T(256)S(1)}, u32[]{:S(2)}) copy-start(f32[256]{0:T(256)S(1)} %broadcast_multiply_fusion.1) | copy-start | bytes 3076
  1467.4 371.4 %reduce-scatter.16.cloned.1.call-start = ((), (), s32[]{:S(2)}) async-start(), calls=%async_computation.17 | async-start | bytes 18874368
  1534.7 314.4 %reduce-scatter.18.cloned.1.call-start = ((), (), s32[]{:S(2)}) async-start(), calls=%async_computation.18 | async-start | bytes 18874368
  1603.4 285.4 %reduce-scatter.14.cloned.1.call-start = ((), (), s32[]{:S(2)}) async-start(), calls=%async_computation.16 | async-start | bytes 18874368 | tf_op jit(solution)/shard_map/reduce_scatter | solution.py:269
  1625.0 421.8 %all-reduce.14.cloned.1.call-start = ((), (), s32[]{:S(2)}) async-start(), calls=%async_computation.19 | async-start | bytes 8388608 | tf_op jit(solution)/shard_map/psum | solution.py:351
  1824.8 295.9 %reduce-scatter.12.cloned.1.call-start = ((), (), s32[]{:S(2)}) async-start(), calls=%async_computation.14 | async-start | bytes 9437184 | tf_op jit(solution)/shard_map/reduce_scatter | solution.py:333
  1836.6 414.6 %all-reduce.12.cloned.1.call-start = ((), (), s32[]{:S(2)}) async-start(), calls=%async_computation.15 | async-start | bytes 262144 | tf_op jit(solution)/shard_map/psum | solution.py:354
  2046.8 76.4 %copy-start.8 = (f32[256,2048]{1,0:T(8,128)S(1)}, f32[256,2048]{1,0:T(8,128)}, u32[]{:S(2)}) copy-start(f32[256,2048]{1,0:T(8,128)} %copy-done.6) | copy-start | bytes 6291460
  2046.8 76.4 %copy-start.42 = (f32[2048]{0:T(1024)S(1)}, f32[2048]{0:T(1024)}, u32[]{:S(2)}) copy-start(f32[2048]{0:T(1024)} %param.27) | copy-start | bytes 24580
  2046.8 76.4 %copy-start.54 = (f32[256]{0:T(256)S(1)}, f32[256]{0:T(256)}, u32[]{:S(2)}) copy-start(f32[256]{0:T(256)} %copy-done.52) | copy-start | bytes 3076
  2046.8 76.4 %copy-start.62 = (f32[256]{0:T(256)S(1)}, f32[256]{0:T(256)}, u32[]{:S(2)}) copy-start(f32[256]{0:T(256)} %copy-done.61) | copy-start | bytes 3076
  (71 other events, 442.6 us)
Sparse Core Ops, SparseCore 0:
  103.2 118.8 reduce-scatter.9
  224.0 93.0 all-gather.4
  319.0 93.0 all-gather.6
  413.8 89.7 all-gather.8
  1467.5 52.3 all-gather.10
  1534.8 114.4 reduce-scatter.15
  1652.8 116.1 reduce-scatter.17
  1772.6 116.1 reduce-scatter.13
  1891.8 154.9 all-reduce.13
  2050.1 70.4 reduce-scatter.11
  2126.8 124.4 all-reduce.11
where the time goes:
time: 2270 us; the launch traced here: 2260 us
  waiting for transfers between devices  1360 us (60%)
  matrix products  361 us (16%)
  local copies, waits for them, and re-layouts  310 us (14%)
  other arithmetic  145 us (6%)
  blocking collectives  39.8 us (2%)
  starting transfers between devices  26.5 us (1%)
    all_to_all x1, waiting for transfers between devices, body(): lax.all_to_all(send_in.reshape(layout), 'expert', split_axis=0, concat_ax...  248 us
    all_to_all x1, waiting for transfers between devices, body(): lax.all_to_all(grad_inputs, 'expert', split_axis=0, concat_axis=0, tiled=...  240 us
    all_to_all x1, waiting for transfers between devices, body(): lax.all_to_all(send_grad.reshape(layout), 'expert', split_axis=0, concat_...  227 us
    all_to_all x1, waiting for transfers between devices, body(): lax.all_to_all(expert_out, 'expert', split_axis=0, concat_axis=0, tiled=T...  216 us
    psum x1, waiting for transfers between devices, body(): lax.psum(qkv_part.astype(jnp.bfloat16), 'expert').astype(jnp.float32)  154 us
    unnamed x156, local copies, waits for them, and re-layouts  146 us
    reduce_scatter x1, waiting for transfers between devices, body(): lax.psum_scatter(jnp.dot(row_part, w_out, preferred_element_type=jnp.floa...  96.5 us
    psum x1, waiting for transfers between devices, body(): lax.psum((attn_gain_part, q_gain_part, k_gain_part, ffn_gain_part, router...  82.2 us
  transfers between devices with their start and end apart: 15, of which 9 were waited for; matrix products, arithmetic and copies ran while one was open for 26% of the time, Pallas kernels for 0%

commit v1 on v0

v1 whole, which is shorter than its diff:
```python
import functools
import math

import jax
import jax.numpy as jnp
from jax import lax
from jax.experimental import pallas as pl
from jax.experimental.pallas import tpu as pltpu
from jax.sharding import PartitionSpec as P

NORM_EPS = 1e-06
ROPE_BASE = 50000.0
F32 = jnp.float32
BF16 = jnp.bfloat16
NT = (((1,), (1,)), ((), ()))
TN = (((0,), (0,)), ((), ()))
CORE, NEAR, FAR = 1, 2, 4
VMEM_LIMIT = 60 * 1024 * 1024


def params(**kw):
    return pltpu.CompilerParams(vmem_limit_bytes=VMEM_LIMIT, **kw)


def cost(flops, nbytes, trans=0):
    return pl.CostEstimate(flops=int(flops), bytes_accessed=int(nbytes), transcendentals=int(trans))


def full(shape):
    return pl.BlockSpec(shape, lambda *_: (0,) * len(shape))


def rms_scale(values):
    return lax.rsqrt(jnp.mean(values * values, axis=-1, keepdims=True) + NORM_EPS)


def project_kernel(x, gain, w, cos, sin, q_gain, k_gain, normed, q, k, v, raw, *, heads, width):
    xf = x[...].astype(F32)
    low = (xf * rms_scale(xf) * gain[...]).astype(BF16)
    normed[...] = low
    proj = jnp.dot(low, w[...], preferred_element_type=F32)
    span = heads * width
    raw[...] = proj[:, : 2 * span]
    v[...] = proj[:, 2 * span :].astype(BF16)
    c, s = cos[...], sin[...]
    for part, (out, head_gain) in enumerate(((q, q_gain), (k, k_gain))):
        for h in range(heads):
            u = proj[:, part * span + h * width : part * span + (h + 1) * width]
            u = u * rms_scale(u) * head_gain[...]
            out[:, h * width : (h + 1) * width] = (
                u * c + pltpu.roll(u, width // 2, 1) * s
            ).astype(BF16)


def project(x, gain, w, cos, sin, q_gain, k_gain, heads, width):
    rows, depth = x.shape
    span = heads * width
    blk = min(256, rows)
    row = lambda n: pl.BlockSpec((blk, n), lambda i: (i, 0))
    return pl.pallas_call(
        functools.partial(project_kernel, heads=heads, width=width),
        grid=(rows // blk,),
        in_specs=[row(depth), full((1, depth)), full(w.shape), row(width), row(width), full((1, width)), full((1, width))],
        out_specs=[row(depth), row(span), row(span), row(span), row(2 * span)],
        out_shape=[
            jax.ShapeDtypeStruct((rows, depth), BF16),
            jax.ShapeDtypeStruct((rows, span), BF16),
            jax.ShapeDtypeStruct((rows, span), BF16),
            jax.ShapeDtypeStruct((rows, span), BF16),
            jax.ShapeDtypeStruct((rows, 2 * span), F32),
        ],
        compiler_params=params(),
        cost_estimate=cost(2 * rows * depth * 3 * span, rows * depth * 4 + w.size * 2 + rows * span * 14),
        name="project",
    )(x, gain[None], w, cos, sin, q_gain[None], k_gain[None])


def attend_kernel(lo, hi, seg_col, seg_row, q, k, v, out, lse, s_sc, *, scale, blk):
    i = pl.program_id(1)
    first, last = lo[i], hi[i]
    qb, sr = q[...], seg_row[...]

    def at(j):
        return pl.ds(pl.multiple_of(j * blk, blk), blk)

    def scores(j, peak):
        s = lax.dot_general(k[at(j), :], qb, NT, preferred_element_type=F32) * scale
        s = jnp.where(seg_col[at(j), :] == sr, s, -1e30)
        s_sc[at(j), :] = s
        return jnp.maximum(peak, jnp.max(s, axis=0, keepdims=True))

    peak = lax.fori_loop(first, last, scores, jnp.full((1, blk), -1e30, F32))

    def weights(j, total):
        e = jnp.exp(s_sc[at(j), :] - peak)
        s_sc[at(j), :] = e
        return total + jnp.sum(e, axis=0, keepdims=True)

    total = lax.fori_loop(first, last, weights, jnp.zeros((1, blk), F32))
    inv = 1.0 / total

    def mix(j, acc):
        p = (s_sc[at(j), :] * inv).astype(BF16)
        return acc + lax.dot_general(v[at(j), :], p, TN, preferred_element_type=F32)

    acc = lax.fori_loop(first, last, mix, jnp.zeros((v.shape[1], blk), F32))
    out[...] = acc.T.astype(BF16)
    lse[0] = peak + jnp.log(total)


def attend(q, k, v, seg, lo, hi, heads, width, scale):
    rows = q.shape[0]
    blk = min(256, rows)
    head = pl.BlockSpec((rows, width), lambda h, i, *_: (0, h))
    tile = pl.BlockSpec((blk, width), lambda h, i, *_: (i, h))
    return pl.pallas_call(
        functools.partial(attend_kernel, scale=scale, blk=blk),
        grid_spec=pltpu.PrefetchScalarGridSpec(
            num_scalar_prefetch=2,
            grid=(heads, rows // blk),
            in_specs=[full((rows, 1)), pl.BlockSpec((1, blk), lambda h, i, *_: (0, i)), tile, head, head],
            out_specs=[tile, pl.BlockSpec((1, 1, blk), lambda h, i, *_: (h, 0, i))],
            scratch_shapes=[pltpu.VMEM((rows, blk), F32)],
        ),
        out_shape=[
            jax.ShapeDtypeStruct((rows, heads * width), BF16),
            jax.ShapeDtypeStruct((heads, 1, rows), F32),
        ],
        compiler_params=params(),
        cost_estimate=cost(2 * heads * rows * rows * width, heads * rows * width * 8, heads * rows * rows // 2),
        name="attend",
    )(lo, hi, seg[:, None], seg[None, :], q, k, v)


def attend_back_kernel(lo, hi, seg_col, seg_row, lse, q, k, v, g, dq, dk, dv, p_sc, d_sc, *, scale, blk):
    i = pl.program_id(1)
    first, last = lo[i], hi[i]
    qb, gb, sr, total = q[...], g[...], seg_row[...], lse[0]

    @pl.when(i == 0)
    def _():
        dk[...] = jnp.zeros_like(dk)
        dv[...] = jnp.zeros_like(dv)

    def at(j):
        return pl.ds(pl.multiple_of(j * blk, blk), blk)

    def forward(j, delta):
        s = lax.dot_general(k[at(j), :], qb, NT, preferred_element_type=F32) * scale
        s = jnp.where(seg_col[at(j), :] == sr, s, -1e30)
        p = jnp.exp(s - total)
        d = lax.dot_general(v[at(j), :], gb, NT, preferred_element_type=F32)
        p_sc[at(j), :] = p
        d_sc[at(j), :] = d
        return delta + jnp.sum(p * d, axis=0, keepdims=True)

    delta = lax.fori_loop(first, last, forward, jnp.zeros((1, blk), F32))

    def backward(j, acc):
        p = p_sc[at(j), :]
        ds = (p * (d_sc[at(j), :] - delta)).astype(BF16)
        dv[at(j), :] += jnp.dot(p.astype(BF16), gb, preferred_element_type=F32)
        dk[at(j), :] += jnp.dot(ds, qb, preferred_element_type=F32) * scale
        return acc + lax.dot_general(k[at(j), :], ds, TN, preferred_element_type=F32)

    acc = lax.fori_loop(first, last, backward, jnp.zeros((q.shape[1], blk), F32))
    dq[...] = acc.T * scale


def attend_back(q, k, v, g, lse, seg, lo, hi, heads, width, scale):
    rows = q.shape[0]
    blk = min(256, rows)
    head = pl.BlockSpec((rows, width), lambda h, i, *_: (0, h))
    tile = pl.BlockSpec((blk, width), lambda h, i, *_: (i, h))
    shape = jax.ShapeDtypeStruct((rows, heads * width), F32)
    return pl.pallas_call(
        functools.partial(attend_back_kernel, scale=scale, blk=blk),
        grid_spec=pltpu.PrefetchScalarGridSpec(
            num_scalar_prefetch=2,
            grid=(heads, rows // blk),
            in_specs=[
                full((rows, 1)),
                pl.BlockSpec((1, blk), lambda h, i, *_: (0, i)),
                pl.BlockSpec((1, 1, blk), lambda h, i, *_: (h, 0, i)),
                tile, head, head, tile,
            ],
            out_specs=[tile, head, head],
            scratch_shapes=[pltpu.VMEM((rows, blk), F32)] * 2,
        ),
        out_shape=[shape] * 3,
        compiler_params=params(),
        cost_estimate=cost(5 * heads * rows * rows * width, heads * rows * width * 20, heads * rows * rows // 2),
        name="attend_back",
    )(lo, hi, seg[:, None], seg[None, :], lse, q, k, v, g)


def shape_back_kernel(dq, dk, dv, raw, cos, sin, q_gain, k_gain, out, gq, gk, *, heads, width):
    span = heads * width
    c, s = cos[...], sin[...]

    @pl.when(pl.program_id(0) == 0)
    def _():
        gq[...] = jnp.zeros_like(gq)
        gk[...] = jnp.zeros_like(gk)

    for part, (grad, head_gain, gain_sum) in enumerate(((dq, q_gain, gq), (dk, k_gain, gk))):
        for h in range(heads):
            y = grad[:, h * width : (h + 1) * width]
            x = raw[:, part * span + h * width : part * span + (h + 1) * width]
            r = rms_scale(x)
            du = y * c - pltpu.roll(y, width // 2, 1) * s
            gain_sum[...] += jnp.sum(du * x * r, axis=0, keepdims=True)
            scaled = du * head_gain[...]
            back = r * (scaled - x * r * r * jnp.mean(scaled * x, axis=-1, keepdims=True))
            out[:, part * span + h * width : part * span + (h + 1) * width] = back.astype(BF16)
    out[:, 2 * span :] = dv[...].astype(BF16)


def shape_back(dq, dk, dv, raw, cos, sin, q_gain, k_gain, heads, width):
    rows, span = dq.shape
    blk = min(256, rows)
    row = lambda n: pl.BlockSpec((blk, n), lambda i: (i, 0))
    return pl.pallas_call(
        functools.partial(shape_back_kernel, heads=heads, width=width),
        grid=(rows // blk,),
        in_specs=[row(span), row(span), row(span), row(2 * span), row(width), row(width), full((1, width)), full((1, width))],
        out_specs=[row(3 * span), full((1, width)), full((1, width))],
        out_shape=[
            jax.ShapeDtypeStruct((rows, 3 * span), BF16),
            jax.ShapeDtypeStruct((1, width), F32),
            jax.ShapeDtypeStruct((1, width), F32),
        ],
        compiler_params=params(),
        cost_estimate=cost(rows * span * 60, rows * span * 30),
        name="shape_back",
    )(dq, dk, dv, raw, cos, sin, q_gain[None], k_gain[None])


def expert_kernel(*refs, pieces, unit, expert, first):
    x, g, gates = refs[:3]
    gu_hbm, d_hbm = refs[3 : 3 + pieces], refs[3 + pieces : 3 + 2 * pieces]
    outs = refs[3 + 2 * pieces :]
    hg, hg_t, dgu, dgates = outs[:4]
    x_t = outs[4] if first else None
    gu_w, d_w, sems = outs[-3:]

    @pl.when(pl.program_id(0) == 0)
    def _():
        copies = []
        for s in range(pieces):
            copies.append(pltpu.make_async_copy(gu_hbm[s], gu_w.at[:, s * 2 * unit : (s + 1) * 2 * unit], sems.at[2 * s]))
            copies.append(pltpu.make_async_copy(d_hbm[s], d_w.at[s * unit : (s + 1) * unit, :], sems.at[2 * s + 1]))
        for copy in copies:
            copy.start()
        for copy in copies:
            copy.wait()

    xb = x[...]
    gate = gates[:, expert : expert + 1]
    both = jnp.dot(xb, gu_w[...], preferred_element_type=F32)
    back = lax.dot_general(g[...], d_w[...], NT, preferred_element_type=F32)
    acc = jnp.zeros((xb.shape[0], unit), F32)
    for s in range(pieces):
        pre = both[:, 2 * s * unit : (2 * s + 1) * unit]
        up = both[:, (2 * s + 1) * unit : (2 * s + 2) * unit]
        t = back[:, s * unit : (s + 1) * unit]
        sig = 1.0 / (1.0 + jnp.exp(-pre))
        act = pre * sig
        hid = (act * up).astype(BF16).astype(F32)
        acc = acc + hid * t
        dh = gate * t
        dgu[:, 2 * s * unit : (2 * s + 1) * unit] = (dh * up * sig * (1.0 + pre * (1.0 - sig))).astype(BF16)
        dgu[:, (2 * s + 1) * unit : (2 * s + 2) * unit] = (dh * act).astype(BF16)
        low = (gate * hid).astype(BF16)
        hg[:, s * unit : (s + 1) * unit] = low
        hg_t[s * unit : (s + 1) * unit, :] = low.T
    dgates[...] = jnp.sum(acc, axis=1, keepdims=True)
    if first:
        x_t[...] = xb.T


def expert_forward(x, g, gates, gu, d, expert, first):
    rows, depth = x.shape
    pieces, unit = len(gu), d[0].shape[0]
    hidden = pieces * unit
    blk = min(256, rows)
    row = lambda n: pl.BlockSpec((blk, n), lambda i: (i, 0))
    any_spec = pl.BlockSpec(memory_space=pl.ANY)
    out_specs = [row(hidden), pl.BlockSpec((hidden, blk), lambda i: (0, i)), row(2 * hidden), row(1)]
    out_shape = [
        jax.ShapeDtypeStruct((rows, hidden), BF16),
        jax.ShapeDtypeStruct((hidden, rows), BF16),
        jax.ShapeDtypeStruct((rows, 2 * hidden), BF16),
        jax.ShapeDtypeStruct((rows, 1), F32),
    ]
    if first:
        out_specs.append(pl.BlockSpec((depth, blk), lambda i: (0, i)))
        out_shape.append(jax.ShapeDtypeStruct((depth, rows), BF16))
    return pl.pallas_call(
        functools.partial(expert_kernel, pieces=pieces, unit=unit, expert=expert, first=first),
        grid=(rows // blk,),
        in_specs=[row(depth), row(depth), row(gates.shape[1])] + [any_spec] * (2 * pieces),
        out_specs=out_specs,
        out_shape=out_shape,
        scratch_shapes=[
            pltpu.VMEM((depth, 2 * hidden), BF16),
            pltpu.VMEM((hidden, depth), BF16),
            pltpu.SemaphoreType.DMA((2 * pieces,)),
        ],
        compiler_params=params(),
        cost_estimate=cost(6 * rows * depth * hidden, rows * depth * 4 + hidden * depth * 6 + rows * hidden * 8),
        name=f"expert_forward_{expert}",
    )(x, g, gates, *gu, *d)


def input_back_kernel(*refs, experts, pieces):
    grads, weights, out = refs[:experts], refs[experts:-1], refs[-1]
    left = jnp.concatenate([r[...] for r in grads], axis=1)
    right = jnp.concatenate([r[...] for r in weights], axis=1)
    out[...] = lax.dot_general(left, right, NT, preferred_element_type=F32).astype(BF16)


def input_back(grads, weights, chunk, rows):
    experts, pieces = len(grads), len(weights[0])
    depth, wide = weights[0][0].shape
    cols = min(512, depth)
    return pl.pallas_call(
        functools.partial(input_back_kernel, experts=experts, pieces=pieces),
        grid=(depth // cols,),
        in_specs=[pl.BlockSpec((rows, grads[0].shape[1]), lambda j: (chunk, 0))] * experts
        + [pl.BlockSpec((cols, wide), lambda j: (j, 0))] * (experts * pieces),
        out_specs=pl.BlockSpec((rows, cols), lambda j: (0, j)),
        out_shape=jax.ShapeDtypeStruct((rows, depth), BF16),
        compiler_params=params(),
        cost_estimate=cost(2 * rows * depth * experts * pieces * wide, experts * pieces * wide * (depth + rows) * 2 + rows * depth * 2),
        name=f"input_back_{chunk}",
    )(*grads, *[w for per in weights for w in per])


def output_sum_kernel(*refs, experts):
    hidden, weights, out = refs[:experts], refs[experts:-1], refs[-1]
    left = jnp.concatenate([r[...] for r in hidden], axis=1)
    right = jnp.concatenate([r[...] for r in weights], axis=0)
    out[...] = jnp.dot(left, right, preferred_element_type=F32).astype(BF16)


def output_sum(hidden, weights):
    experts, pieces = len(hidden), len(weights[0])
    rows = hidden[0].shape[0]
    unit, depth = weights[0][0].shape
    cols, blk = min(512, depth), min(512, rows)
    return pl.pallas_call(
        functools.partial(output_sum_kernel, experts=experts),
        grid=(depth // cols, rows // blk),
        in_specs=[pl.BlockSpec((blk, hidden[0].shape[1]), lambda j, i: (i, 0))] * experts
        + [pl.BlockSpec((unit, cols), lambda j, i: (0, j))] * (experts * pieces),
        out_specs=pl.BlockSpec((blk, cols), lambda j, i: (i, j)),
        out_shape=jax.ShapeDtypeStruct((rows, depth), BF16),
        compiler_params=params(),
        cost_estimate=cost(2 * rows * depth * experts * pieces * unit, experts * pieces * unit * (depth + rows) * 2 + rows * depth * 2),
        name="output_sum",
    )(*hidden, *[w for per in weights for w in per])


def weight_back_kernel(x_t, dgu, hg_t, g, *outs, pieces, unit):
    gu = jnp.dot(x_t[...], dgu[...], preferred_element_type=F32).astype(BF16)
    d = jnp.dot(hg_t[...], g[...], preferred_element_type=F32).astype(BF16)
    for s in range(pieces):
        outs[s][...] = gu[:, 2 * s * unit : 2 * (s + 1) * unit]
        outs[pieces + s][...] = d[s * unit : (s + 1) * unit, :]


def weight_back(x_t, dgu, hg_t, g, pieces, expert):
    depth, rows = x_t.shape
    hidden = hg_t.shape[0]
    unit = hidden // pieces
    blk = min(256, depth)
    outs = pl.pallas_call(
        functools.partial(weight_back_kernel, pieces=pieces, unit=unit),
        grid=(depth // blk,),
        in_specs=[
            pl.BlockSpec((blk, rows), lambda i: (i, 0)),
            full(dgu.shape),
            full(hg_t.shape),
            pl.BlockSpec((rows, blk), lambda i: (0, i)),
        ],
        out_specs=[pl.BlockSpec((blk, 2 * unit), lambda i: (i, 0))] * pieces
        + [pl.BlockSpec((unit, blk), lambda i: (0, i))] * pieces,
        out_shape=[jax.ShapeDtypeStruct((depth, 2 * unit), BF16)] * pieces
        + [jax.ShapeDtypeStruct((unit, depth), BF16)] * pieces,
        compiler_params=params(),
        cost_estimate=cost(6 * rows * depth * hidden, rows * depth * 4 + hidden * depth * 6 + rows * hidden * 6),
        name=f"weight_back_{expert}",
    )(x_t, dgu, hg_t, g)
    return list(outs[:pieces]), list(outs[pieces:])


def swap(value, mask):
    size = lax.axis_size("tensor")
    return lax.ppermute(value, "tensor", [(i, i ^ mask) for i in range(size)])


def chain_gather(value):
    size = lax.axis_size("expert")
    here = lax.axis_index("expert")
    ups, downs = [value], [value]
    for k in range(size - 1):
        ups.append(lax.ppermute(ups[-1], "expert", [(i, i + 1) for i in range(k, size - 1)]))
        downs.append(lax.ppermute(downs[-1], "expert", [(i + 1, i) for i in range(size - 1 - k)]))
    return [value] + [jnp.where(here >= s, ups[s], downs[size - s]) for s in range(1, size)]


def send_back(value, step):
    size = lax.axis_size("expert")
    if step == 0:
        return value
    return lax.ppermute(value, "expert", [(i, (i - step) % size) for i in range(size)])


def all_sum(value):
    for axis in ("tensor", "expert"):
        size = lax.axis_size(axis)
        bit = 1
        while bit < size:
            value = value + lax.ppermute(value, axis, [(i, i ^ bit) for i in range(size)])
            bit *= 2
    return value


def chain_sum(value):
    size = lax.axis_size("expert")
    here = lax.axis_index("expert")
    rows, columns = value.shape
    part = rows // size
    low = value.astype(BF16)
    total = lax.dynamic_slice_in_dim(value, here * part, part, 0).astype(BF16).astype(F32)
    for s in range(1, size):
        piece = lax.dynamic_slice_in_dim(low, ((here - s) % size) * part, part, 0)
        total = total + send_back(piece, s).astype(F32)
    total = total.astype(BF16)
    out = jnp.zeros((rows, columns), F32)
    for s, piece in enumerate(chain_gather(total)):
        out = lax.dynamic_update_slice(out, piece.astype(F32), (((here - s) % size) * part, 0))
    return out


def tie(values, after):
    return lax.optimization_barrier((values, after))[0]


def experts_dense(ffn_in, gates_all, grads, w_gate, w_up, w_down, after):
    own, depth = ffn_in.shape
    here = lax.axis_index("expert")
    size = lax.axis_size("expert")
    count, _, unit = w_gate.shape
    gu, down = [], []
    for e in range(count):
        pack = (jnp.concatenate([w_gate[e], w_up[e]], axis=1), w_down[e])
        if e > 0:
            pack = tie(pack, after)
        near = [swap(v, NEAR) for v in pack]
        far = [swap(v, FAR) for v in pack]
        both = [swap(v, FAR) for v in near] if e % 2 == 0 else [swap(v, NEAR) for v in far]
        gu.append([pack[0], near[0], far[0], both[0]])
        down.append([pack[1], near[1], far[1], both[1]])
    rows = []
    for piece in chain_gather(ffn_in):
        rows += [piece, swap(piece, CORE)]
    x = jnp.concatenate(rows, axis=0)
    pair = jnp.stack([gates_all, swap(gates_all, CORE)])
    pair = lax.dynamic_slice_in_dim(jnp.concatenate(chain_gather(pair), axis=0).reshape(2 * size * own, -1), here * count, count, 1)
    hidden, hidden_t, pre_grads, gate_grads, x_t = [], [], [], [], None
    weight_grads = []
    for e in range(count):
        out = expert_forward(x, grads, pair, gu[e], down[e], e, e == 0)
        if e == 0:
            x_t = out[4]
        hidden.append(out[0])
        hidden_t.append(out[1])
        pre_grads.append(out[2])
        gate_grads.append(out[3])
    back = jnp.concatenate(gate_grads, axis=1).reshape(size, 2, own, count)
    back = back[:, 0] + swap(back[:, 1], CORE)
    back = jnp.stack([send_back(back[s], s) for s in range(size)])
    twice = jnp.concatenate([back, back], axis=0)
    by_index = lax.dynamic_slice_in_dim(twice, size - here, size, 0)
    grad_gates = by_index.transpose(1, 0, 2).reshape(own, size * count)

    def to_owner(chunk, s):
        mine = chunk[:own].astype(F32) + swap(chunk[own:], CORE).astype(F32)
        return send_back(mine.astype(BF16), s)

    order = list(range(1, size)) + [0]
    grad_rows = 0.0
    for s in order:
        grad_rows = grad_rows + to_owner(input_back(pre_grads, gu, s, 2 * own), s).astype(F32)
    for e in range(count):
        weight_grads.append(weight_back(x_t, pre_grads[e], hidden_t[e], grads, len(gu[e]), e))
    mixed = output_sum(hidden, down)
    mixture = 0.0
    for s in order:
        mixture = mixture + to_owner(mixed[2 * own * s : 2 * own * (s + 1)], s).astype(F32)
    sums_gu, sums_d = [], []
    for e, (p_gu, p_d) in enumerate(weight_grads):
        first, second = (2, 1) if e % 2 == 0 else (1, 2)
        results = []
        for p in (p_gu, p_d):
            late = (p[second].astype(F32) + swap(p[3], (NEAR, FAR)[first - 1]).astype(F32)).astype(BF16)
            got_first = swap(p[first], (NEAR, FAR)[first - 1])
            got_second = swap(late, (NEAR, FAR)[second - 1])
            results.append(p[0].astype(F32) + got_first.astype(F32) + got_second.astype(F32))
        sums_gu.append(results[0])
        sums_d.append(results[1])
    grad_gate = jnp.stack([v[:, :unit] for v in sums_gu])
    grad_up = jnp.stack([v[:, unit:] for v in sums_gu])
    grad_down = jnp.stack(sums_d)
    return mixture, grad_gates, grad_rows, grad_gate, grad_up, grad_down


def swiglu_back(grad_hidden, gate_pre, up_pre):
    sigmoid = jax.nn.sigmoid(gate_pre)
    grad_gate = grad_hidden * up_pre * sigmoid * (1.0 + gate_pre * (1.0 - sigmoid))
    grad_up = grad_hidden * gate_pre * sigmoid
    return (grad_gate.astype(BF16), grad_up.astype(BF16))


def experts_routed(ffn_in, gate_weights, routes, grad_output, w_gate, w_up, w_down, experts_all, capacity):
    own_rows, model_width = ffn_in.shape
    top_count = routes.shape[1]
    experts_here = w_gate.shape[0]
    senders = lax.axis_size("expert")
    flat_routes = routes.reshape(-1)
    expert_hits = (flat_routes[:, None] == jnp.arange(experts_all, dtype=jnp.int32)[None, :]).astype(jnp.int32)
    slot_index = jnp.sum(expert_hits * (jnp.cumsum(expert_hits, axis=0) - 1), axis=1)
    spread_in = jnp.broadcast_to(ffn_in[:, None, :], (own_rows, top_count, model_width)).reshape(-1, model_width)
    spread_grad = (gate_weights[:, :, None] * grad_output[:, None, :]).astype(BF16).reshape(-1, model_width)
    empty = jnp.zeros((experts_all, capacity, model_width), BF16)
    layout = (senders, experts_here, capacity, model_width)
    exchange = functools.partial(lax.all_to_all, axis_name="expert", split_axis=0, concat_axis=0, tiled=True)
    recv_rows = exchange(empty.at[flat_routes, slot_index].set(spread_in).reshape(layout))
    expert_grad = exchange(empty.at[flat_routes, slot_index].set(spread_grad).reshape(layout))
    gate_full = lax.all_gather(w_gate, "tensor", axis=2, tiled=True)
    up_full = lax.all_gather(w_up, "tensor", axis=2, tiled=True)
    down_full = lax.all_gather(w_down, "tensor", axis=1, tiled=True)
    dot = functools.partial(jnp.einsum, preferred_element_type=F32)
    gate_all = dot("sctd,cdf->sctf", recv_rows, gate_full)
    up_all = dot("sctd,cdf->sctf", recv_rows, up_full)
    hidden_low = (jax.nn.silu(gate_all) * up_all).astype(BF16)
    expert_out = dot("sctf,cfd->sctd", hidden_low, down_full).astype(BF16)
    grad_hidden = dot("sctd,cfd->sctf", expert_grad, down_full)
    grad_gate_pre, grad_up_pre = swiglu_back(grad_hidden, gate_all, up_all)
    whole_down = dot("sctf,sctd->cfd", hidden_low, expert_grad)
    whole_gate = dot("sctd,sctf->cdf", recv_rows, grad_gate_pre)
    whole_up = dot("sctd,sctf->cdf", recv_rows, grad_up_pre)
    grad_inputs = (dot("sctf,cdf->sctd", grad_gate_pre, gate_full) + dot("sctf,cdf->sctd", grad_up_pre, up_full)).astype(BF16)

    def scatter(whole, dim):
        return lax.psum_scatter(whole.astype(BF16), "tensor", scatter_dimension=dim, tiled=True).astype(F32)

    pick_index = flat_routes * capacity + slot_index

    def picked(values):
        return (
            exchange(values).reshape(experts_all * capacity, model_width)[pick_index]
            .reshape(own_rows, top_count, model_width).astype(F32)
        )

    rows_back, grads_back = picked(expert_out), picked(grad_inputs)
    mixture = jnp.sum(gate_weights[:, :, None] * rows_back, axis=1)
    grad_gates = jnp.sum(grad_output[:, None, :] * rows_back, axis=-1)
    return mixture, grad_gates, jnp.sum(grads_back, axis=1), scatter(whole_gate, 2), scatter(whole_up, 2), scatter(whole_down, 1)


def body(
    layer_input, cotangent, lengths, routes, attn_gain, w_qkv, q_gain, k_gain, w_out, ffn_gain, w_router, w_gate, w_up, w_down,
):
    group_rows, model_width = layer_input.shape
    own_rows, top_count = routes.shape
    width = q_gain.shape[0]
    heads = w_qkv.shape[2] // width
    span = heads * width
    experts_all = w_router.shape[1]
    ranks = lax.axis_size("tensor")
    rank = lax.axis_index("tensor")
    capacity = max(2, 3 * own_rows * top_count // (2 * experts_all))
    dense = 2 * own_rows <= 3 * capacity and ranks == 8
    scale = 1.0 / math.sqrt(width)

    if dense:
        grads = []
        for piece in chain_gather(cotangent):
            grads += [piece, swap(piece, CORE)]
        grads = jnp.concatenate(grads, axis=0)
    out_weight = lax.all_gather(w_out, "tensor", axis=0, tiled=True)

    seq_lengths = lengths[0]
    ends = jnp.cumsum(seq_lengths)
    starts = ends - seq_lengths
    index = jnp.arange(group_rows, dtype=jnp.int32)
    segment = jnp.sum((index[:, None] >= ends[None, :]).astype(jnp.int32), axis=1)
    offset = jnp.max(jnp.where(index[:, None] >= starts[None, :], starts[None, :], 0), axis=1)
    position = index - offset
    blk = min(256, group_rows)
    tops = jnp.arange(group_rows // blk, dtype=jnp.int32) * blk
    lo = jnp.max(jnp.where(tops[:, None] >= starts[None, :], starts[None, :], 0), axis=1) // blk
    tails = tops + blk - 1
    hi = jnp.min(jnp.where(tails[:, None] < ends[None, :], ends[None, :], group_rows), axis=1)
    hi = (hi + blk - 1) // blk
    half = width // 2
    frequency = jnp.exp(jnp.arange(half, dtype=F32) * (-2.0 * math.log(ROPE_BASE) / width))
    angle = position.astype(F32)[:, None] * frequency[None, :]
    cosine, sine = jnp.cos(angle), jnp.sin(angle)
    cosine = jnp.concatenate([cosine, cosine], axis=1)
    sine = jnp.concatenate([-sine, sine], axis=1)

    qkv_weight = w_qkv.reshape(model_width, 3 * span)
    normed, q, k, v, raw = project(layer_input, attn_gain, qkv_weight, cosine, sine, q_gain, k_gain, heads, width)
    mixed, lse = attend(q, k, v, segment, lo, hi, heads, width, scale)

    mixed_own = lax.all_to_all(mixed.reshape(ranks, own_rows, span), "tensor", split_axis=0, concat_axis=0, tiled=True)
    mixed_own = mixed_own.transpose(1, 0, 2).reshape(own_rows, ranks * span)
    input_own = lax.dynamic_slice_in_dim(layer_input, rank * own_rows, own_rows, 0).astype(F32)
    scale_own = rms_scale(input_own)
    residual = input_own + jnp.dot(mixed_own, out_weight, preferred_element_type=F32)
    scale_two = rms_scale(residual)
    ffn_in = (residual * scale_two * ffn_gain).astype(BF16)
    logits = jnp.dot(ffn_in, w_router, preferred_element_type=F32)
    probabilities = jax.nn.softmax(logits, axis=-1)
    chosen = routes[:, :, None] == jnp.arange(experts_all, dtype=jnp.int32)[None, None, :]
    grad_output = cotangent.astype(F32)
    if dense:
        any_chosen = jnp.any(chosen, axis=1)
        gates_all = jnp.where(any_chosen, probabilities, 0.0)
        mixture, grad_gates, grad_rows, grad_gate, grad_up, grad_down = experts_dense(
            ffn_in, gates_all, grads, w_gate, w_up, w_down, mixed_own
        )
        grad_probs = jnp.where(any_chosen, grad_gates, 0.0)
    else:
        gate_weights = jnp.sum(jnp.where(chosen, probabilities[:, None, :], 0.0), axis=-1)
        mixture, grad_gates, grad_rows, grad_gate, grad_up, grad_down = experts_routed(
            ffn_in, gate_weights, routes, grad_output, w_gate, w_up, w_down, experts_all, capacity
        )
        grad_probs = jnp.sum(jnp.where(chosen, grad_gates[:, :, None], 0.0), axis=1)
    output = (residual + mixture).astype(BF16)
    grad_logits = (
        probabilities * (grad_probs - jnp.sum(grad_probs * probabilities, axis=-1, keepdims=True))
    ).astype(BF16)
    router_part = lax.dot_general(ffn_in, grad_logits, TN, preferred_element_type=F32)
    grad_ffn = grad_rows + lax.dot_general(grad_logits, w_router, NT, preferred_element_type=F32)
    ffn_gain_part = jnp.sum(grad_ffn * residual * scale_two, axis=0)
    scaled_two = grad_ffn * ffn_gain
    grad_residual = grad_output + scale_two * (
        scaled_two - residual * scale_two * scale_two * jnp.mean(scaled_two * residual, axis=-1, keepdims=True)
    )
    grad_attn = grad_residual.astype(BF16)

    grad_mixed = lax.dot_general(grad_attn, out_weight, NT, preferred_element_type=F32).astype(BF16)
    grad_mixed = grad_mixed.reshape(own_rows, ranks, span).transpose(1, 0, 2)
    grad_mixed = lax.all_to_all(grad_mixed, "tensor", split_axis=0, concat_axis=0, tiled=True).reshape(group_rows, span)
    grad_attn_all = lax.all_gather(grad_attn, "tensor", axis=0, tiled=True)
    out_part = lax.dot_general(mixed, grad_attn_all, TN, preferred_element_type=F32)
    grad_q, grad_k, grad_v = attend_back(q, k, v, grad_mixed, lse, segment, lo, hi, heads, width, scale)
    grad_qkv, q_gain_part, k_gain_part = shape_back(grad_q, grad_k, grad_v, raw, cosine, sine, q_gain, k_gain, heads, width)
    qkv_part = lax.dot_general(normed, grad_qkv, TN, preferred_element_type=F32)
    grad_normed = lax.psum_scatter(
        lax.dot_general(grad_qkv, qkv_weight, NT, preferred_element_type=F32).astype(BF16),
        "tensor", scatter_dimension=0, tiled=True,
    ).astype(F32)
    attn_gain_part = jnp.sum(qkv_weight.astype(F32) * qkv_part, axis=1) / attn_gain
    scaled_one = grad_normed * attn_gain
    grad_input = grad_residual + scale_own * (
        scaled_one - input_own * scale_own * scale_own * jnp.mean(scaled_one * input_own, axis=-1, keepdims=True)
    )
    grad_out_sum = chain_sum(out_part)
    grad_qkv_sum = chain_sum(qkv_part).reshape(w_qkv.shape)
    early = all_sum(jnp.concatenate([router_part.T, ffn_gain_part[None]], axis=0))
    late = all_sum(jnp.concatenate([attn_gain_part[None], jnp.pad(jnp.concatenate([q_gain_part, k_gain_part], axis=1), ((0, 0), (0, model_width - 2 * width)))], axis=0))
    return (
        output,
        grad_input.astype(BF16),
        late[0],
        grad_qkv_sum,
        late[1, :width],
        late[1, width : 2 * width],
        grad_out_sum,
        early[experts_all],
        early[:experts_all].T,
        grad_gate,
        grad_up,
        grad_down,
    )


def solution(mesh):
    in_specs = (
        P("expert", None),
        P(("expert", "tensor"), None),
        P("expert", None),
        P(("expert", "tensor"), None),
        P(),
        P(None, None, "tensor"),
        P(),
        P(),
        P("tensor", None),
        P(),
        P(),
        P("expert", None, "tensor"),
        P("expert", None, "tensor"),
        P("expert", "tensor", None),
    )
    out_specs = (
        P(("expert", "tensor"), None),
        P(("expert", "tensor"), None),
        P(),
        P(None, None, "tensor"),
        P(),
        P(),
        P("tensor", None),
        P(),
        P(),
        P("expert", None, "tensor"),
        P("expert", None, "tensor"),
        P("expert", "tensor", None),
    )
    return jax.shard_map(body, mesh=mesh, in_specs=in_specs, out_specs=out_specs, check_vma=False)
```

time: 2270 us -> 1370 us (0.60)
  waiting for transfers between devices: 1360 us -> 478 us
  Pallas kernels: 0 us -> 362 us
  matrix products: 361 us -> 36.7 us
  starting transfers between devices: 26.5 us -> 293 us
  local copies, waits for them, and re-layouts: 310 us -> 84.7 us
  other arithmetic: 145 us -> 91.3 us
  blocking collectives: 39.8 us -> 0 us
    all_to_all x4 -> x2, waiting for transfers between devices: 931 us -> 20.7 us  [the longest x1 13.1 us: body(): lax.all_to_all(grad_mixed, 'tensor', split_axis=0, concat_axis=0, tiled=T...]
    ppermute x0 -> x121, waiting for transfers between devices: none -> 457 us  [the longest x66 246 us: swap(): return lax.ppermute(value, 'tensor', [(i, i ^ mask) for i in range(size)])]
    pallas_call x0 -> x17, Pallas kernels: none -> 362 us  [the longest x4 91.5 us: expert_forward(): pl.pallas_call(functools.partial(expert_kernel, pieces=pieces, unit=unit,...]
    dot_general x46 -> x8, matrix products: 361 us -> 36.7 us  [the longest x1 11.3 us: body(): lax.dot_general(grad_qkv, qkv_weight, NT, preferred_element_type=F32)]
    ppermute x0 -> x121, starting transfers between devices: none -> 283 us  [the longest x15 109 us: chain_gather(): lax.ppermute(ups[-1], 'expert', [(i, i + 1) for i in range(k, size - 1)])]
    psum x2 -> x0, waiting for transfers between devices: 236 us -> none  [the longest x1 154 us: body(): lax.psum(qkv_part.astype(jnp.bfloat16), 'expert').astype(jnp.float32)]
    reduce_scatter x3 -> x1, waiting for transfers between devices: 193 us -> 0.01 us  [body(): lax.psum_scatter(lax.dot_general(grad_qkv, qkv_weight, NT, preferred_elem...]
    unnamed x156 -> x151, local copies, waits for them, and re-layouts: 146 us -> 35.3 us
  transfers between devices with their start and end apart: 15 -> 126, of which waited for: 9 -> 42; matrix products, arithmetic and copies ran while one was open for 26% -> 15% of each run, Pallas kernels for 0% -> 25%
where the time goes in v1:
time: 1370 us; the launch traced here: 1360 us
  waiting for transfers between devices  478 us (35%)
  Pallas kernels  362 us (26%)
  starting transfers between devices  293 us (21%)
  other arithmetic  91.3 us (7%)
  local copies, waits for them, and re-layouts  84.7 us (6%)
  matrix products  36.7 us (3%)
  between operations  15.4 us (1%)
    ppermute x66, waiting for transfers between devices, swap(): return lax.ppermute(value, 'tensor', [(i, i ^ mask) for i in range(size)])  246 us
    ppermute x15, waiting for transfers between devices, chain_gather(): lax.ppermute(downs[-1], 'expert', [(i + 1, i) for i in range(size - 1 - k)])  125 us
    ppermute x15, starting transfers between devices, chain_gather(): lax.ppermute(ups[-1], 'expert', [(i, i + 1) for i in range(k, size - 1)])  109 us
    pallas_call x4, Pallas kernels, expert_forward(): pl.pallas_call(functools.partial(expert_kernel, pieces=pieces, unit=unit,...  91.5 us
    ppermute x15, starting transfers between devices, send_back(): lax.ppermute(value, 'expert', [(i, (i - step) % size) for i in range(size)])  89.2 us
    pallas_call x4, Pallas kernels, weight_back(): pl.pallas_call(functools.partial(weight_back_kernel, pieces=pieces, unit=...  75.7 us
    ppermute x15, waiting for transfers between devices, send_back(): lax.ppermute(value, 'expert', [(i, (i - step) % size) for i in range(size)])  66.6 us
    pallas_call x4, Pallas kernels, input_back(): pl.pallas_call(functools.partial(input_back_kernel, experts=experts, piec...  56 us
  transfers between devices with their start and end apart: 126, of which 42 were waited for; matrix products, arithmetic and copies ran while one was open for 15% of the time, Pallas kernels for 25%

profile of v1, /device:TPU:0, one launch (start us, length us, event | category | flops | bytes accessed | tf_op | source)
XLA Modules:
  0.0 1360.4 jit_solution(7643955360749734216)
XLA Ops:
  27.5 16.6 %project.1 = (bf16[2048,2048]{1,0:T(8,128)(2,1)}, bf16[2048,256]{1,0:T(8,128)(2,1)}, bf16[2048,256]{1,0:T(8,128)(2,1)}, bf16[2048,256]{1,0:T(8,128)(2,1)}, f32[2048,512]{1,0:T(8,128)}) custom-call(bf16[2048,2048]{1,0:T(8,128)(2,1)} %x.3, f32[1,2048]{1,0:T(1,128)} %bitcast.141, bf16[2048,768]{1,0:T(8,128)(2,1)} %copy.67.w, ...), custom_call_target="tpu_custom_call" | custom-call | flops 6442450944 | bytes 27262976 | tf_op jit(solution)/shard_map/project/pallas_call | solution.py:60
  45.4 38.6 %attend.1 = (bf16[2048,256]{1,0:T(8,128)(2,1)}, f32[2,1,2048]{2,1,0:T(1,128)}) custom-call(s32[8]{0:T(128)} %get-tuple-element.263.lo, s32[8]{0:T(128)} %get-tuple-element.262.hi, s32[2048,1]{1,0:T(8,128)} %copy.68.seg_col, s32[1,2048]{1,0:T(1,128)} %bitcast.147, bf16[2048,256]{1,0:T(8,128)(2,1)} %get-tuple-element.80.q, ...), custom_call_target="tpu_custom_call" | custom-call | flops 2147483648 | bytes 4194304 | tf_op jit(solution)/shard_map/attend/pallas_call | solution.py:116
  135.2 15.8 %collective-permute-done.2 = bf16[256,2048]{1,0:T(8,128)(2,1)} collective-permute-done((bf16[256,2048]{1,0:T(8,128)(2,1)S(1)}, bf16[256,2048]{1,0:T(8,128)(2,1)}, u32[]{:S(2)}, u32[]{:S(2)}) %collective-permute-start.2) | collective-permute-done | bytes 1048608 | tf_op jit(solution)/shard_map/ppermute | solution.py:409
  188.6 14.4 %collective-permute-done.4 = bf16[256,2048]{1,0:T(8,128)(2,1)S(1)} collective-permute-done((bf16[256,2048]{1,0:T(8,128)(2,1)}, bf16[256,2048]{1,0:T(8,128)(2,1)S(1)}, u32[]{:S(2)}, u32[]{:S(2)}) %collective-permute-start.4) | collective-permute-done | bytes 1048608 | tf_op jit(solution)/shard_map/ppermute | solution.py:409
  258.0 38.0 %collective-permute-start.21 = (f32[2,256,16]{1,2,0:T(8,128)S(1)}, f32[2,256,16]{1,2,0:T(8,128)S(1)}, u32[]{:S(2)}, u32[]{:S(2)}) collective-permute-start(f32[2,256,16]{1,2,0:T(8,128)S(1)} %pad_maximum_fusion.10), channel_id=1, source_target_pairs={{0,8},{8,16},{16,24},{1,9},{9,17},{17,25},{2,10},{10,18},{18,26},{... | collective-permute-start | bytes 98312 | tf_op jit(solution)/shard_map/ppermute | solution.py:408
  324.1 52.6 %collective-permute-done.50.refs_10_.refs_19_ = bf16[128,2048]{1,0:T(8,128)(2,1)} collective-permute-done((bf16[128,2048]{1,0:T(8,128)(2,1)}, bf16[128,2048]{1,0:T(8,128)(2,1)}, u32[]{:S(2)}, u32[]{:S(2)}) %collective-permute-start.50) | collective-permute-done | bytes 524320 | tf_op jit(solution)/shard_map/ppermute | solution.py:400
  379.2 22.6 %expert_forward_3.1 = (bf16[2048,512]{1,0:T(8,128)(2,1)}, bf16[512,2048]{1,0:T(8,128)(2,1)}, bf16[2048,1024]{1,0:T(8,128)(2,1)}, f32[2048,1]{1,0:T(8,128)}) custom-call(bf16[2048,2048]{1,0:T(8,128)(2,1)} %constant_dynamic-update-slice_fusion.refs_0_, bf16[2048,2048]{1,0:T(8,128)(2,1)} %constant_dynamic-update-slice_fusion.8.refs_1_.g, ...), custom_call_target="tpu_custom_call" | custom-call | flops 12884901888 | bytes 31457280 | tf_op jit(solution)/shard_map/expert_forward_3/pallas_call | solution.py:299
  406.0 15.3 %collective-permute-done.41.refs_6_.refs_15_ = bf16[2048,256]{1,0:T(8,128)(2,1)} collective-permute-done((bf16[2048,256]{1,0:T(8,128)(2,1)}, bf16[2048,256]{1,0:T(8,128)(2,1)}, u32[]{:S(2)}, u32[]{:S(2)}) %collective-permute-start.41) | collective-permute-done | bytes 1048608 | tf_op jit(solution)/shard_map/ppermute | solution.py:400
  421.9 22.6 %expert_forward_2.1 = (bf16[2048,512]{1,0:T(8,128)(2,1)}, bf16[512,2048]{1,0:T(8,128)(2,1)}, bf16[2048,1024]{1,0:T(8,128)(2,1)}, f32[2048,1]{1,0:T(8,128)}) custom-call(bf16[2048,2048]{1,0:T(8,128)(2,1)} %constant_dynamic-update-slice_fusion.refs_0_, bf16[2048,2048]{1,0:T(8,128)(2,1)} %constant_dynamic-update-slice_fusion.8.refs_1_.g, ...), custom_call_target="tpu_custom_call" | custom-call | flops 12884901888 | bytes 31457280 | tf_op jit(solution)/shard_map/expert_forward_2/pallas_call | solution.py:299
  445.3 16.8 %collective-permute-done.36.refs_8_.refs_9_ = bf16[128,2048]{1,0:T(8,128)(2,1)} collective-permute-done((bf16[128,2048]{1,0:T(8,128)(2,1)S(1)}, bf16[128,2048]{1,0:T(8,128)(2,1)}, u32[]{:S(2)}, u32[]{:S(2)}) %collective-permute-start.36) | collective-permute-done | bytes 524320 | tf_op jit(solution)/shard_map/ppermute | solution.py:400
  474.7 16.3 %collective-permute-done.35.refs_6_.refs_11_ = bf16[2048,256]{1,0:T(8,128)(2,1)} collective-permute-done((bf16[2048,256]{1,0:T(8,128)(2,1)}, bf16[2048,256]{1,0:T(8,128)(2,1)}, u32[]{:S(2)}, u32[]{:S(2)}) %collective-permute-start.35) | collective-permute-done | bytes 1048608 | tf_op jit(solution)/shard_map/ppermute | solution.py:400
  491.0 22.6 %expert_forward_1.1 = (bf16[2048,512]{1,0:T(8,128)(2,1)}, bf16[512,2048]{1,0:T(8,128)(2,1)}, bf16[2048,1024]{1,0:T(8,128)(2,1)}, f32[2048,1]{1,0:T(8,128)}) custom-call(bf16[2048,2048]{1,0:T(8,128)(2,1)} %constant_dynamic-update-slice_fusion.refs_0_, bf16[2048,2048]{1,0:T(8,128)(2,1)} %constant_dynamic-update-slice_fusion.8.refs_1_.g, ...), custom_call_target="tpu_custom_call" | custom-call | flops 12884901888 | bytes 31457280 | tf_op jit(solution)/shard_map/expert_forward_1/pallas_call | solution.py:299
  518.4 23.6 %expert_forward_0.1 = (bf16[2048,512]{1,0:T(8,128)(2,1)}, bf16[512,2048]{1,0:T(8,128)(2,1)}, bf16[2048,1024]{1,0:T(8,128)(2,1)}, f32[2048,1]{1,0:T(8,128)}, bf16[2048,2048]{1,0:T(8,128)(2,1)}) custom-call(bf16[2048,2048]{1,0:T(8,128)(2,1)} %constant_dynamic-update-slice_fusion.refs_0_, bf16[2048,2048]{1,0:T(8,128)(2,1)} %constant_dynamic-update-slice_fusion.8.refs_1_.g, ...), custom_call_target="tpu_custom_call" | custom-call | flops 12884901888 | bytes 31457280 | tf_op jit(solution)/shard_map/expert_forward_0/pallas_call | solution.py:299
  543.7 14.0 %input_back_0.1 = bf16[512,2048]{1,0:T(8,128)(2,1)} custom-call(bf16[2048,1024]{1,0:T(8,128)(2,1)} %get-tuple-element.94.refs_0_.dgu, bf16[2048,1024]{1,0:T(8,128)(2,1)} %get-tuple-element.95.refs_1_.dgu, bf16[2048,1024]{1,0:T(8,128)(2,1)} %get-tuple-element.96.refs_2_.dgu, bf16[2048,1024]{1,0:T(8,128)(2,1)} %get-tuple-element.97.refs_3_.dgu, ...), custom_call_target="tpu_custom_call" | custom-call | flops 8589934592 | bytes 23068672 | tf_op jit(solution)/shard_map/input_back_0/pallas_call | solution.py:327
  576.8 14.1 %input_back_2.1 = bf16[512,2048]{1,0:T(8,128)(2,1)} custom-call(bf16[2048,1024]{1,0:T(8,128)(2,1)} %get-tuple-element.94.refs_0_.dgu, bf16[2048,1024]{1,0:T(8,128)(2,1)} %get-tuple-element.95.refs_1_.dgu, bf16[2048,1024]{1,0:T(8,128)(2,1)} %get-tuple-element.96.refs_2_.dgu, bf16[2048,1024]{1,0:T(8,128)(2,1)} %get-tuple-element.97.refs_3_.dgu, ...), custom_call_target="tpu_custom_call" | custom-call | flops 8589934592 | bytes 23068672 | tf_op jit(solution)/shard_map/input_back_2/pallas_call | solution.py:327
  610.0 18.8 %weight_back_3.1 = (bf16[2048,256]{1,0:T(8,128)(2,1)}, bf16[2048,256]{1,0:T(8,128)(2,1)}, bf16[2048,256]{1,0:T(8,128)(2,1)}, bf16[2048,256]{1,0:T(8,128)(2,1)}, ...) custom-call(bf16[2048,2048]{1,0:T(8,128)(2,1)} %get-tuple-element.11, ...), custom_call_target="tpu_custom_call" | custom-call | flops 12884901888 | bytes 29360128 | tf_op jit(solution)/shard_map/weight_back_3/pallas_call | solution.py:378
  646.5 19.1 %weight_back_2.1 = (bf16[2048,256]{1,0:T(8,128)(2,1)}, bf16[2048,256]{1,0:T(8,128)(2,1)}, bf16[2048,256]{1,0:T(8,128)(2,1)}, bf16[2048,256]{1,0:T(8,128)(2,1)}, ...) custom-call(bf16[2048,2048]{1,0:T(8,128)(2,1)} %get-tuple-element.11, ...), custom_call_target="tpu_custom_call" | custom-call | flops 12884901888 | bytes 29360128 | tf_op jit(solution)/shard_map/weight_back_2/pallas_call | solution.py:378
  669.9 41.9 %collective-permute-done.61 = bf16[256,2048]{1,0:T(8,128)(2,1)} collective-permute-done((bf16[256,2048]{1,0:T(8,128)(2,1)}, bf16[256,2048]{1,0:T(8,128)(2,1)}, u32[]{:S(2)}, u32[]{:S(2)}) %collective-permute-start.61) | collective-permute-done | bytes 1048608 | tf_op jit(solution)/shard_map/ppermute | solution.py:417
  719.5 18.8 %weight_back_1.1 = (bf16[2048,256]{1,0:T(8,128)(2,1)}, bf16[2048,256]{1,0:T(8,128)(2,1)}, bf16[2048,256]{1,0:T(8,128)(2,1)}, bf16[2048,256]{1,0:T(8,128)(2,1)}, ...) custom-call(bf16[2048,2048]{1,0:T(8,128)(2,1)} %get-tuple-element.11, ...), custom_call_target="tpu_custom_call" | custom-call | flops 12884901888 | bytes 29360128 | tf_op jit(solution)/shard_map/weight_back_1/pallas_call | solution.py:378
  738.3 19.0 %weight_back_0.1 = (bf16[2048,256]{1,0:T(8,128)(2,1)}, bf16[2048,256]{1,0:T(8,128)(2,1)}, bf16[2048,256]{1,0:T(8,128)(2,1)}, bf16[2048,256]{1,0:T(8,128)(2,1)}, ...) custom-call(bf16[2048,2048]{1,0:T(8,128)(2,1)} %get-tuple-element.11, ...), custom_call_target="tpu_custom_call" | custom-call | flops 12884901888 | bytes 29360128 | tf_op jit(solution)/shard_map/weight_back_0/pallas_call | solution.py:378
  757.2 29.3 %output_sum.1 = bf16[2048,2048]{1,0:T(8,128)(2,1)} custom-call(bf16[2048,512]{1,0:T(8,128)(2,1)} %get-tuple-element.84.refs_0_, bf16[2048,512]{1,0:T(8,128)(2,1)} %get-tuple-element.87.refs_1_, bf16[2048,512]{1,0:T(8,128)(2,1)} %get-tuple-element.90.refs_2_, bf16[2048,512]{1,0:T(8,128)(2,1)} %get-tuple-element.93.refs_3_, ...), custom_call_target="tpu_custom_call" | custom-call | flops 17179869184 | bytes 25165824 | tf_op jit(solution)/shard_map/output_sum/pallas_call | solution.py:352
  806.9 20.9 %collective-permute-done.113 = bf16[128,2048]{1,0:T(8,128)(2,1)S(1)} collective-permute-done((bf16[128,2048]{1,0:T(8,128)(2,1)S(1)}, bf16[128,2048]{1,0:T(8,128)(2,1)S(1)}, u32[]{:S(2)}, u32[]{:S(2)}) %collective-permute-start.113) | collective-permute-done | bytes 524320 | tf_op jit(solution)/shard_map/ppermute | solution.py:400
  881.8 16.8 %collective-permute-done.98 = bf16[2048,256]{1,0:T(8,128)(2,1)S(1)} collective-permute-done((bf16[2048,256]{1,0:T(8,128)(2,1)S(1)}, bf16[2048,256]{1,0:T(8,128)(2,1)S(1)}, u32[]{:S(2)}, u32[]{:S(2)}) %collective-permute-start.98) | collective-permute-done | bytes 1048608 | tf_op jit(solution)/shard_map/ppermute | solution.py:400
  936.1 43.3 %attend_back.1 = (f32[2048,256]{1,0:T(8,128)}, f32[2048,256]{1,0:T(8,128)}, f32[2048,256]{1,0:T(8,128)}) custom-call(s32[8]{0:T(128)} %get-tuple-element.263.lo, s32[8]{0:T(128)} %get-tuple-element.262.hi, s32[2048,1]{1,0:T(8,128)} %copy.68.seg_col, s32[1,2048]{1,0:T(1,128)} %bitcast.148, f32[2,1,2048]{2,1,0:T(1,128)} %get-tuple-element.102.lse, ...), custom_call_target="tpu_custom_call" | custom-call | flops 5368709120 | bytes 10485760 | tf_op jit(solution)/shard_map/attend_back/pallas_call | solution.py:176
  1009.9 17.7 %collective-permute-done.100 = bf16[2048,256]{1,0:T(8,128)(2,1)S(1)} collective-permute-done((bf16[2048,256]{1,0:T(8,128)(2,1)}, bf16[2048,256]{1,0:T(8,128)(2,1)S(1)}, u32[]{:S(2)}, u32[]{:S(2)}) %collective-permute-start.100) | collective-permute-done | bytes 1048608 | tf_op jit(solution)/shard_map/ppermute | solution.py:400
  1027.6 17.6 %collective-permute-done.102 = bf16[2048,256]{1,0:T(8,128)(2,1)S(1)} collective-permute-done((bf16[2048,256]{1,0:T(8,128)(2,1)S(1)}, bf16[2048,256]{1,0:T(8,128)(2,1)S(1)}, u32[]{:S(2)}, u32[]{:S(2)}) %collective-permute-start.102) | collective-permute-done | bytes 1048608 | tf_op jit(solution)/shard_map/ppermute | solution.py:400
  1059.0 42.6 %collective-permute-start.76 = (bf16[512,768]{0,1:T(8,128)(2,1)S(1)}, bf16[512,768]{0,1:T(8,128)(2,1)S(1)}, u32[]{:S(2)}, u32[]{:S(2)}) collective-permute-start(bf16[512,768]{0,1:T(8,128)(2,1)S(1)} %get-tuple-element.219), channel_id=1, source_target_pairs={{0,8},{8,16},{16,24},{24,0},{1,9},{9,17},{17,25},{25,1},{2,10},{10... | collective-permute-start | bytes 2359304 | tf_op jit(solution)/shard_map/ppermute | solution.py:417
  1141.3 24.9 %collective-permute-start.77 = (bf16[512,768]{0,1:T(8,128)(2,1)S(1)}, bf16[512,768]{0,1:T(8,128)(2,1)S(1)}, u32[]{:S(2)}, u32[]{:S(2)}) collective-permute-start(bf16[512,768]{0,1:T(8,128)(2,1)S(1)} %get-tuple-element.191), channel_id=1, source_target_pairs={{0,8},{8,16},{16,24},{1,9},{9,17},{17,25},{2,10},{10,18},{18,26},{... | collective-permute-start | bytes 2359304 | tf_op jit(solution)/shard_map/ppermute | solution.py:408
  1242.1 14.8 %collective-permute-start.54 = (bf16[256,2048]{1,0:T(8,128)(2,1)}, bf16[256,2048]{1,0:T(8,128)(2,1)}, u32[]{:S(2)}, u32[]{:S(2)}) collective-permute-start(bf16[256,2048]{1,0:T(8,128)(2,1)} %get-tuple-element.215), channel_id=1, source_target_pairs={{0,16},{8,24},{16,0},{24,8},{1,17},{9,25},{17,1},{25,9},{2,18},{10... | collective-permute-start | bytes 3145736 | tf_op jit(solution)/shard_map/ppermute | solution.py:417
  1271.4 22.4 %collective-permute-start.86 = (bf16[64,2048]{1,0:T(8,128)(2,1)}, bf16[64,2048]{1,0:T(8,128)(2,1)S(1)}, u32[]{:S(2)}, u32[]{:S(2)}) collective-permute-start(bf16[64,2048]{1,0:T(8,128)(2,1)} %get-tuple-element.189), channel_id=1, source_target_pairs={{0,8},{8,16},{16,24},{1,9},{9,17},{17,25},{2,10},{10,18},{18,26},{... | collective-permute-start | bytes 786440 | tf_op jit(solution)/shard_map/ppermute | solution.py:408
  1293.8 17.4 %collective-permute-done.87 = bf16[64,2048]{1,0:T(8,128)(2,1)S(1)} collective-permute-done((bf16[64,2048]{1,0:T(8,128)(2,1)}, bf16[64,2048]{1,0:T(8,128)(2,1)S(1)}, u32[]{:S(2)}, u32[]{:S(2)}) %collective-permute-start.87) | collective-permute-done | bytes 262176 | tf_op jit(solution)/shard_map/ppermute | solution.py:409
  1313.4 30.6 %collective-permute-done.88 = bf16[64,2048]{1,0:T(8,128)(2,1)S(1)} collective-permute-done((bf16[64,2048]{1,0:T(8,128)(2,1)S(1)}, bf16[64,2048]{1,0:T(8,128)(2,1)S(1)}, u32[]{:S(2)}, u32[]{:S(2)}) %collective-permute-start.88) | collective-permute-done | bytes 262176 | tf_op jit(solution)/shard_map/ppermute | solution.py:409
  (530 shorter events, 585.0 us)
Async XLA Ops:
  7.2 99.9 %all-gather.3.cloned.1.call-start = ((), (), s32[]{:S(2)}) async-start(), calls=%async_computation.3 | async-start | bytes 9437184 | tf_op jit(solution)/shard_map/all_gather | solution.py:594
  91.7 1125.5 %all-gather.5.cloned.1.call-start = ((), (), s32[]{:S(2)}) async-start(), calls=%async_computation.5 | async-start | bytes 9437184 | tf_op jit(solution)/shard_map/all_gather | solution.py:660
  164.1 67.8 %collective-permute-start.30 = (bf16[128,2048]{1,0:T(8,128)(2,1)}, bf16[128,2048]{1,0:T(8,128)(2,1)}, u32[]{:S(2)}, u32[]{:S(2)}) collective-permute-start(bf16[128,2048]{1,0:T(8,128)(2,1)} %get-tuple-element.233.refs_7_.refs_4_), channel_id=1, source_target_pairs={{0,2},{1,3},{2,0},{3,1},{4,6},{5,7},{6,4},{7,5},{8,10},{9,11},{10,... | collective-permute-start | bytes 1572872 | tf_op jit(solution)/shard_map/ppermute | solution.py:400
  228.3 69.7 %collective-permute-start.46 = (bf16[2048,256]{1,0:T(8,128)(2,1)S(1)}, bf16[2048,256]{1,0:T(8,128)(2,1)}, u32[]{:S(2)}, u32[]{:S(2)}) collective-permute-start(bf16[2048,256]{1,0:T(8,128)(2,1)S(1)} %pad_maximum_fusion.8.refs_3_.refs_16_), channel_id=1, source_target_pairs={{0,4},{1,5},{2,6},{3,7},{4,0},{5,1},{6,2},{7,3},{8,12},{9,13},{10,... | collective-permute-start | bytes 3145736 | tf_op jit(solution)/shard_map/ppermute | solution.py:400
  231.9 65.4 %collective-permute-start.42 = (bf16[128,2048]{1,0:T(8,128)(2,1)}, bf16[128,2048]{1,0:T(8,128)(2,1)}, u32[]{:S(2)}, u32[]{:S(2)}) collective-permute-start(bf16[128,2048]{1,0:T(8,128)(2,1)} %get-tuple-element.89.refs_7_.refs_12_), channel_id=1, source_target_pairs={{0,2},{1,3},{2,0},{3,1},{4,6},{5,7},{6,4},{7,5},{8,10},{9,11},{10,... | collective-permute-start | bytes 1572872 | tf_op jit(solution)/shard_map/ppermute | solution.py:400
  240.9 62.9 %collective-permute-start.9 = (bf16[256,2048]{1,0:T(8,128)(2,1)}, bf16[256,2048]{1,0:T(8,128)(2,1)}, u32[]{:S(2)}, u32[]{:S(2)}) collective-permute-start(bf16[256,2048]{1,0:T(8,128)(2,1)} %get-tuple-element.202), channel_id=1, source_target_pairs={{0,1},{1,0},{2,3},{3,2},{4,5},{5,4},{6,7},{7,6},{8,9},{9,8},{10,11... | collective-permute-start | bytes 3145736 | tf_op jit(solution)/shard_map/ppermute | solution.py:400
  297.9 79.3 %collective-permute-start.39 = (bf16[2048,256]{1,0:T(8,128)(2,1)}, bf16[2048,256]{1,0:T(8,128)(2,1)}, u32[]{:S(2)}, u32[]{:S(2)}) collective-permute-start(bf16[2048,256]{1,0:T(8,128)(2,1)} %get-tuple-element.88.refs_3_.refs_12_), channel_id=1, source_target_pairs={{0,2},{1,3},{2,0},{3,1},{4,6},{5,7},{6,4},{7,5},{8,10},{9,11},{10,... | collective-permute-start | bytes 3145736 | tf_op jit(solution)/shard_map/ppermute | solution.py:400
  299.4 79.3 %collective-permute-start.47 = (bf16[2048,256]{1,0:T(8,128)(2,1)}, bf16[2048,256]{1,0:T(8,128)(2,1)}, u32[]{:S(2)}, u32[]{:S(2)}) collective-permute-start(bf16[2048,256]{1,0:T(8,128)(2,1)} %collective-permute-done.46.refs_5_.refs_18_), channel_id=1, source_target_pairs={{0,2},{1,3},{2,0},{3,1},{4,6},{5,7},{6,4},{7,5},{8,10},{9,11},{10,... | collective-permute-start | bytes 3145736 | tf_op jit(solution)/shard_map/ppermute | solution.py:400
  303.8 72.9 %collective-permute-start.50 = (bf16[128,2048]{1,0:T(8,128)(2,1)}, bf16[128,2048]{1,0:T(8,128)(2,1)}, u32[]{:S(2)}, u32[]{:S(2)}) collective-permute-start(bf16[128,2048]{1,0:T(8,128)(2,1)} %collective-permute-done.49.refs_9_.refs_18_), channel_id=1, source_target_pairs={{0,2},{1,3},{2,0},{3,1},{4,6},{5,7},{6,4},{7,5},{8,10},{9,11},{10,... | collective-permute-start | bytes 1572872 | tf_op jit(solution)/shard_map/ppermute | solution.py:400
  315.3 87.0 %collective-permute-start.40 = (bf16[2048,256]{1,0:T(8,128)(2,1)}, bf16[2048,256]{1,0:T(8,128)(2,1)}, u32[]{:S(2)}, u32[]{:S(2)}) collective-permute-start(bf16[2048,256]{1,0:T(8,128)(2,1)} %get-tuple-element.88.refs_3_.refs_12_), channel_id=1, source_target_pairs={{0,4},{1,5},{2,6},{3,7},{4,0},{5,1},{6,2},{7,3},{8,12},{9,13},{10,... | collective-permute-start | bytes 3145736 | tf_op jit(solution)/shard_map/ppermute | solution.py:400
  323.5 80.8 %collective-permute-start.34 = (bf16[2048,256]{1,0:T(8,128)(2,1)}, bf16[2048,256]{1,0:T(8,128)(2,1)}, u32[]{:S(2)}, u32[]{:S(2)}) collective-permute-start(bf16[2048,256]{1,0:T(8,128)(2,1)} %get-tuple-element.85.refs_3_.refs_8_), channel_id=1, source_target_pairs={{0,4},{1,5},{2,6},{3,7},{4,0},{5,1},{6,2},{7,3},{8,12},{9,13},{10,... | collective-permute-start | bytes 3145736 | tf_op jit(solution)/shard_map/ppermute | solution.py:400
  404.3 68.9 %collective-permute-start.38 = (bf16[128,2048]{1,0:T(8,128)(2,1)}, bf16[128,2048]{1,0:T(8,128)(2,1)}, u32[]{:S(2)}, u32[]{:S(2)}) collective-permute-start(bf16[128,2048]{1,0:T(8,128)(2,1)} %collective-permute-done.37.refs_9_.refs_10_), channel_id=1, source_target_pairs={{0,2},{1,3},{2,0},{3,1},{4,6},{5,7},{6,4},{7,5},{8,10},{9,11},{10,... | collective-permute-start | bytes 1572872 | tf_op jit(solution)/shard_map/ppermute | solution.py:400
  421.4 69.6 %collective-permute-start.35 = (bf16[2048,256]{1,0:T(8,128)(2,1)}, bf16[2048,256]{1,0:T(8,128)(2,1)}, u32[]{:S(2)}, u32[]{:S(2)}) collective-permute-start(bf16[2048,256]{1,0:T(8,128)(2,1)} %collective-permute-done.34.refs_5_.refs_10_), channel_id=1, source_target_pairs={{0,2},{1,3},{2,0},{3,1},{4,6},{5,7},{6,4},{7,5},{8,10},{9,11},{10,... | collective-permute-start | bytes 3145736 | tf_op jit(solution)/shard_map/ppermute | solution.py:400
  444.6 73.7 %collective-permute-start.28 = (bf16[2048,256]{1,0:T(8,128)(2,1)S(1)}, bf16[2048,256]{1,0:T(8,128)(2,1)}, u32[]{:S(2)}, u32[]{:S(2)}) collective-permute-start(bf16[2048,256]{1,0:T(8,128)(2,1)S(1)} %copy-done.3), channel_id=1, source_target_pairs={{0,4},{1,5},{2,6},{3,7},{4,0},{5,1},{6,2},{7,3},{8,12},{9,13},{10,... | collective-permute-start | bytes 3145736 | tf_op jit(solution)/shard_map/ppermute | solution.py:400
  543.6 85.3 %collective-permute-start.65 = (f32[4,256,4]{1,2,0:T(4,128)S(1)}, f32[4,256,4]{1,2,0:T(4,128)S(1)}, u32[]{:S(2)}, u32[]{:S(2)}) collective-permute-start(f32[4,256,4]{1,2,0:T(4,128)S(1)} %bitcast.149), channel_id=1, source_target_pairs={{0,1},{1,0},{2,3},{3,2},{4,5},{5,4},{6,7},{7,6},{8,9},{9,8},{10,11... | collective-permute-start | bytes 49160 | tf_op jit(solution)/shard_map/ppermute | solution.py:400
  560.0 106.6 %collective-permute-start.64 = (bf16[256,2048]{1,0:T(8,128)(2,1)}, bf16[256,2048]{1,0:T(8,128)(2,1)S(1)}, u32[]{:S(2)}, u32[]{:S(2)}) collective-permute-start(bf16[256,2048]{1,0:T(8,128)(2,1)} %slice.215), channel_id=1, source_target_pairs={{0,1},{1,0},{2,3},{3,2},{4,5},{5,4},{6,7},{7,6},{8,9},{9,8},{10,11... | collective-permute-start | bytes 3145736 | tf_op jit(solution)/shard_map/ppermute | solution.py:400
  642.9 68.9 %collective-permute-start.61 = (bf16[256,2048]{1,0:T(8,128)(2,1)}, bf16[256,2048]{1,0:T(8,128)(2,1)}, u32[]{:S(2)}, u32[]{:S(2)}) collective-permute-start(bf16[256,2048]{1,0:T(8,128)(2,1)} %add_convert_fusion.6), channel_id=1, source_target_pairs={{0,16},{8,24},{16,0},{24,8},{1,17},{9,25},{17,1},{25,9},{2,18},{10... | collective-permute-start | bytes 3145736 | tf_op jit(solution)/shard_map/ppermute | solution.py:417
  645.1 66.8 %collective-permute-start.59 = (bf16[256,2048]{1,0:T(8,128)(2,1)}, bf16[256,2048]{1,0:T(8,128)(2,1)}, u32[]{:S(2)}, u32[]{:S(2)}) collective-permute-start(bf16[256,2048]{1,0:T(8,128)(2,1)} %add_convert_fusion.7), channel_id=1, source_target_pairs={{0,24},{8,0},{16,8},{24,16},{1,25},{9,1},{17,9},{25,17},{2,26},{10... | collective-permute-start | bytes 3145736 | tf_op jit(solution)/shard_map/ppermute | solution.py:417
  665.6 164.2 %collective-permute-start.107 = (bf16[2048,256]{1,0:T(8,128)(2,1)}, bf16[2048,256]{1,0:T(8,128)(2,1)}, u32[]{:S(2)}, u32[]{:S(2)}) collective-permute-start(bf16[2048,256]{1,0:T(8,128)(2,1)} %get-tuple-element.131), channel_id=1, source_target_pairs={{0,2},{1,3},{2,0},{3,1},{4,6},{5,7},{6,4},{7,5},{8,10},{9,11},{10,... | collective-permute-start | bytes 3145736 | tf_op jit(solution)/shard_map/ppermute | solution.py:400
  666.6 166.7 %collective-permute-start.104 = (bf16[2048,256]{1,0:T(8,128)(2,1)}, bf16[2048,256]{1,0:T(8,128)(2,1)}, u32[]{:S(2)}, u32[]{:S(2)}) collective-permute-start(bf16[2048,256]{1,0:T(8,128)(2,1)} %get-tuple-element.126), channel_id=1, source_target_pairs={{0,4},{1,5},{2,6},{3,7},{4,0},{5,1},{6,2},{7,3},{8,12},{9,13},{10,... | collective-permute-start | bytes 3145736 | tf_op jit(solution)/shard_map/ppermute | solution.py:400
  668.2 125.2 %collective-permute-start.119 = (bf16[128,2048]{1,0:T(8,128)(2,1)}, bf16[128,2048]{1,0:T(8,128)(2,1)}, u32[]{:S(2)}, u32[]{:S(2)}) collective-permute-start(bf16[128,2048]{1,0:T(8,128)(2,1)} %get-tuple-element.147), channel_id=1, source_target_pairs={{0,2},{1,3},{2,0},{3,1},{4,6},{5,7},{6,4},{7,5},{8,10},{9,11},{10,... | collective-permute-start | bytes 1572872 | tf_op jit(solution)/shard_map/ppermute | solution.py:400
  791.2 89.3 %collective-permute-start.101 = (bf16[2048,256]{1,0:T(8,128)(2,1)S(1)}, bf16[2048,256]{1,0:T(8,128)(2,1)S(1)}, u32[]{:S(2)}, u32[]{:S(2)}) collective-permute-start(bf16[2048,256]{1,0:T(8,128)(2,1)S(1)} %copy-done.58), channel_id=1, source_target_pairs={{0,2},{1,3},{2,0},{3,1},{4,6},{5,7},{6,4},{7,5},{8,10},{9,11},{10,... | collective-permute-start | bytes 3145736 | tf_op jit(solution)/shard_map/ppermute | solution.py:400
  865.1 406.2 %collective-permute-start.57 = (bf16[256,2048]{1,0:T(8,128)(2,1)}, bf16[256,2048]{1,0:T(8,128)(2,1)}, u32[]{:S(2)}, u32[]{:S(2)}) collective-permute-start(bf16[256,2048]{1,0:T(8,128)(2,1)} %get-tuple-element.209), channel_id=1, source_target_pairs={{0,1},{1,0},{2,3},{3,2},{4,5},{5,4},{6,7},{7,6},{8,9},{9,8},{10,11... | collective-permute-start | bytes 3145736 | tf_op jit(solution)/shard_map/ppermute | solution.py:400
  898.6 102.7 %collective-permute-start.106 = (bf16[2048,256]{1,0:T(8,128)(2,1)}, bf16[2048,256]{1,0:T(8,128)(2,1)}, u32[]{:S(2)}, u32[]{:S(2)}) collective-permute-start(bf16[2048,256]{1,0:T(8,128)(2,1)} %get-tuple-element.129), channel_id=1, source_target_pairs={{0,2},{1,3},{2,0},{3,1},{4,6},{5,7},{6,4},{7,5},{8,10},{9,11},{10,... | collective-permute-start | bytes 3145736 | tf_op jit(solution)/shard_map/ppermute | solution.py:400
  909.3 359.8 %reduce-scatter.2.cloned.1.call-start = ((), (), s32[]{:S(2)}) async-start(), calls=%async_computation.4 | async-start | bytes 9437184 | tf_op jit(solution)/shard_map/reduce_scatter | solution.py:665
  913.7 91.9 %collective-permute-start.103 = (bf16[2048,256]{1,0:T(8,128)(2,1)}, bf16[2048,256]{1,0:T(8,128)(2,1)}, u32[]{:S(2)}, u32[]{:S(2)}) collective-permute-start(bf16[2048,256]{1,0:T(8,128)(2,1)} %get-tuple-element.124), channel_id=1, source_target_pairs={{0,4},{1,5},{2,6},{3,7},{4,0},{5,1},{6,2},{7,3},{8,12},{9,13},{10,... | collective-permute-start | bytes 3145736 | tf_op jit(solution)/shard_map/ppermute | solution.py:400
  915.5 87.7 %collective-permute-start.108 = (bf16[2048,256]{1,0:T(8,128)(2,1)}, bf16[2048,256]{1,0:T(8,128)(2,1)}, u32[]{:S(2)}, u32[]{:S(2)}) collective-permute-start(bf16[2048,256]{1,0:T(8,128)(2,1)} %add_convert_fusion), channel_id=1, source_target_pairs={{0,4},{1,5},{2,6},{3,7},{4,0},{5,1},{6,2},{7,3},{8,12},{9,13},{10,... | collective-permute-start | bytes 3145736 | tf_op jit(solution)/shard_map/ppermute | solution.py:400
  915.7 91.7 %collective-permute-start.105 = (bf16[2048,256]{1,0:T(8,128)(2,1)}, bf16[2048,256]{1,0:T(8,128)(2,1)}, u32[]{:S(2)}, u32[]{:S(2)}) collective-permute-start(bf16[2048,256]{1,0:T(8,128)(2,1)} %add_convert_fusion.1), channel_id=1, source_target_pairs={{0,2},{1,3},{2,0},{3,1},{4,6},{5,7},{6,4},{7,5},{8,10},{9,11},{10,... | collective-permute-start | bytes 3145736 | tf_op jit(solution)/shard_map/ppermute | solution.py:400
  1027.6 81.2 %collective-permute-start.92 = (f32[17,2048]{1,0:T(8,128)S(1)}, f32[17,2048]{1,0:T(8,128)S(1)}, u32[]{:S(2)}, u32[]{:S(2)}) collective-permute-start(f32[17,2048]{1,0:T(8,128)S(1)} %pad_maximum_fusion.9), channel_id=1, source_target_pairs={{0,1},{1,0},{2,3},{3,2},{4,5},{5,4},{6,7},{7,6},{8,9},{9,8},{10,11... | collective-permute-start | bytes 417800 | tf_op jit(solution)/shard_map/ppermute | solution.py:425
  1235.2 110.0 %collective-permute-start.56 = (bf16[256,2048]{1,0:T(8,128)(2,1)}, bf16[256,2048]{1,0:T(8,128)(2,1)}, u32[]{:S(2)}, u32[]{:S(2)}) collective-permute-start(bf16[256,2048]{1,0:T(8,128)(2,1)} %get-tuple-element.214), channel_id=1, source_target_pairs={{0,8},{8,16},{16,24},{24,0},{1,9},{9,17},{17,25},{25,1},{2,10},{10... | collective-permute-start | bytes 3145736 | tf_op jit(solution)/shard_map/ppermute | solution.py:417
  1242.1 103.1 %collective-permute-start.54 = (bf16[256,2048]{1,0:T(8,128)(2,1)}, bf16[256,2048]{1,0:T(8,128)(2,1)}, u32[]{:S(2)}, u32[]{:S(2)}) collective-permute-start(bf16[256,2048]{1,0:T(8,128)(2,1)} %get-tuple-element.215), channel_id=1, source_target_pairs={{0,16},{8,24},{16,0},{24,8},{1,17},{9,25},{17,1},{25,9},{2,18},{10... | collective-permute-start | bytes 3145736 | tf_op jit(solution)/shard_map/ppermute | solution.py:417
  1256.9 88.3 %collective-permute-start.52 = (bf16[256,2048]{1,0:T(8,128)(2,1)S(1)}, bf16[256,2048]{1,0:T(8,128)(2,1)}, u32[]{:S(2)}, u32[]{:S(2)}) collective-permute-start(bf16[256,2048]{1,0:T(8,128)(2,1)S(1)} %copy-done.25), channel_id=1, source_target_pairs={{0,24},{8,0},{16,8},{24,16},{1,25},{9,1},{17,9},{25,17},{2,26},{10... | collective-permute-start | bytes 3145736 | tf_op jit(solution)/shard_map/ppermute | solution.py:417
  (164 other events, 4258.3 us)
Sparse Core Ops, SparseCore 0:
  9.9 57.1 all-gather.2
  719.6 73.8 all-gather.4
  1001.4 109.9 reduce-scatter.1
